TPU v7x, 256 devices: a whole 4x4x8 slice. The times are simulated.
256 devices in a mesh: seq: 64 (over y, z, core), head: 4 (over x).
Axes of the slice: x: 4, y: 4, z: 8, core: 2. Of those that a mesh axis runs over, the one named last changes fastest.
Arguments:
- queries: bfloat16 [32768, 2048], P('seq', 'head'), may hold values from -6 to 6
- keys: bfloat16 [32768, 2048], P('seq', 'head'), may hold values from -6 to 6
- values: bfloat16 [32768, 4096], P('seq', 'head'), may hold values from -6 to 6
- forget_gate: float32 [32768, 8], P('seq', 'head'), may hold values from -1 to 14
- input_gate: float32 [32768, 8], P('seq', 'head'), may hold values from -5 to 215
- out_weight: bfloat16 [4096, 4096], P('head'), may hold values from -0.125 to 0.125
Outputs:
- mixed: bfloat16 [32768, 4096], P('seq', 'head')
- gate_mean: float32 [8], P('head')
All inputs are finite; a program needn't handle non-finite values.
Results may differ from a plain program's by a relative error of at most 0.01.
Values may be sent and summed in bfloat16 or wider, within the bound.
A program may use at most 192 MiB of HBM per device.

v0:
```python
import math

import jax
import jax.numpy as jnp
from jax import lax
from jax.sharding import Mesh
from jax.sharding import PartitionSpec as P

SEQ = ("seq_0", "seq_1", "seq_2")


def filled_with(array, identity):
    return jax.tree.map(
        lambda part, zero: jnp.zeros_like(part) + jnp.asarray(zero, part.dtype), array, identity
    )


def entering(array, axes, combine, identity):
    before = start = filled_with(array, identity)
    so_far = array
    for axis in reversed(axes):
        peers, index = (lax.axis_size(axis), lax.axis_index(axis))
        pieces = jax.tree.map(lambda part: lax.all_gather(part, axis), so_far)
        inside, so_far = (start, start)
        for k in range(peers):
            passed = k < index
            so_far = combine(so_far, jax.tree.map(lambda part: part[k], pieces))
            inside = jax.tree.map(lambda new, old: jnp.where(passed, new, old), so_far, inside)
        before = combine(inside, before)
    return before


def copy_for_each(array, axis):
    copies = jnp.broadcast_to(array, (lax.axis_size(axis), *array.shape))
    return lax.all_to_all(copies, axis, split_axis=0, concat_axis=0, tiled=True)


def taken_together(array, axis):
    return copy_for_each(array, axis).sum(axis=0)


def combine_states(earlier, later_state):
    e_matrix, e_norm, e_max, e_decay = earlier
    l_matrix, l_norm, l_max, l_decay = later_state
    merged_max = jnp.maximum(l_decay + e_max, l_max)
    e_scale = jnp.exp(l_decay + e_max - merged_max)
    l_scale = jnp.exp(l_max - merged_max)
    return (
        e_scale[:, None, None] * e_matrix + l_scale[:, None, None] * l_matrix,
        e_scale[:, None] * e_norm + l_scale[:, None] * l_norm,
        merged_max,
        e_decay + l_decay,
    )


def intra_terms(q_heads, k_heads, v_heads, cum_decay, input_block):
    length = q_heads.shape[0]
    positions = jnp.arange(length)
    causal = positions[:, None] >= positions[None, :]
    log_weight = cum_decay.T[:, :, None] - cum_decay.T[:, None, :] + input_block.T[:, None, :]
    log_weight = jnp.where(causal[None], log_weight, -jnp.inf)
    intra_max = jnp.max(log_weight, axis=2)
    factors = jnp.exp(log_weight - intra_max[:, :, None])
    scores = jnp.einsum(
        "thd,shd->hts", q_heads, k_heads, preferred_element_type=jnp.float32
    ) / math.sqrt(q_heads.shape[2])
    weighted = factors * scores
    intra_den = jnp.sum(weighted, axis=2)
    rounded_weights = weighted.astype(jnp.bfloat16)
    intra_num = jnp.einsum(
        "hts,shv->thv", rounded_weights, v_heads, preferred_element_type=jnp.float32
    )
    return (intra_num, intra_den, intra_max)


def own_terms(k_heads, v_heads, cum_decay, input_block):
    block_decay = cum_decay[-1]
    own_log = block_decay[None, :] - cum_decay + input_block
    own_max = jnp.max(own_log, axis=0)
    key_weight = jnp.exp(own_log - own_max[None, :]) / math.sqrt(k_heads.shape[2])
    weighted_keys = k_heads.astype(jnp.float32) * key_weight[:, :, None]
    own_norm = jnp.sum(weighted_keys, axis=0)
    rounded_keys = weighted_keys.astype(jnp.bfloat16)
    own_matrix = jnp.einsum(
        "shv,shk->hvk", v_heads, rounded_keys, preferred_element_type=jnp.float32
    )
    return (own_matrix, own_norm, own_max, block_decay)


def readout(intra, carried_state, q_heads, cum_decay):
    intra_num, intra_den, intra_max = intra
    carry_matrix, carry_norm, carry_max, unused_decay = carried_state
    carried_log = cum_decay.T + carry_max[:, None]
    stabilizer = jnp.maximum(intra_max, carried_log)
    intra_scale = jnp.exp(intra_max - stabilizer).T
    carry_scale = jnp.exp(carried_log - stabilizer).T
    q_float = q_heads.astype(jnp.float32)
    carried_num = jnp.einsum("hvk,thk->thv", carry_matrix, q_float, precision=lax.Precision.HIGHEST)
    carried_den = jnp.einsum("hk,thk->th", carry_norm, q_float, precision=lax.Precision.HIGHEST)
    numerator = intra_scale[:, :, None] * intra_num + carry_scale[:, :, None] * carried_num
    denominator = intra_scale * intra_den.T + carry_scale * carried_den
    return (numerator / jnp.maximum(jnp.abs(denominator), 1.0)[:, :, None]).astype(jnp.bfloat16)


def shards(queries, keys, values, forget_gate, input_gate, out_weight):
    token_count = queries.shape[0]
    head_count = forget_gate.shape[1]
    qk_width = queries.shape[1] // head_count
    v_width = values.shape[1] // head_count
    q_heads = queries.reshape(token_count, head_count, qk_width)
    k_heads = keys.reshape(token_count, head_count, qk_width)
    v_heads = values.reshape(token_count, head_count, v_width)
    cum_decay = jnp.cumsum(jax.nn.log_sigmoid(forget_gate), axis=0)
    own_state = own_terms(k_heads, v_heads, cum_decay, input_gate)
    identity = (
        jnp.zeros((head_count, v_width, qk_width), jnp.float32),
        jnp.zeros((head_count, qk_width), jnp.float32),
        jnp.full((head_count,), -1e30, jnp.float32),
        jnp.zeros((head_count,), jnp.float32),
    )
    carried_state = entering(own_state, SEQ, combine_states, identity)
    intra = intra_terms(q_heads, k_heads, v_heads, cum_decay, input_gate)
    hidden = readout(intra, carried_state, q_heads, cum_decay).reshape(
        token_count, head_count * v_width
    )
    partial_value = jnp.dot(hidden, out_weight, preferred_element_type=jnp.float32)
    mixed = lax.psum_scatter(
        partial_value.astype(jnp.bfloat16), "head", scatter_dimension=1, tiled=True
    )
    gate_total = taken_together(jnp.sum(input_gate, axis=0), SEQ)
    gate_mean = gate_total / (token_count * lax.axis_size(SEQ))
    return (mixed, gate_mean)


def solution(mesh):
    torus = Mesh(
        mesh.devices.reshape(4, 8, 2, mesh.shape["head"]), ("seq_0", "seq_1", "seq_2", "head")
    )
    placed = (
        P(SEQ, "head"),
        P(SEQ, "head"),
        P(SEQ, "head"),
        P(SEQ, "head"),
        P(SEQ, "head"),
        P("head", None),
    )
    return jax.shard_map(
        shards, mesh=torus, in_specs=placed, out_specs=(P(SEQ, "head"), P("head")), check_vma=False
    )
```

profile of v0, /device:TPU:1, one launch (start us, length us, event | category | flops | bytes accessed | tf_op | source)
XLA Modules:
  0.0 294.9 jit_solution(9901684000675645184)
XLA Ops:
  9.2 1.3 copy.62
  10.5 1.7 copy.60
  12.9 1.3 copy.50
  15.8 4.6 %all-gather.2 = f32[2,1,2]{2,1,0:T(1,128)S(1)} all-gather(f32[1,1,2]{2,1,0:T(1,128)S(1)} %bitcast.677), channel_id=1, replica_groups=mesh['seq_0'=4,'seq_1'=8,'seq_2'=2,'head'=4] {'seq_2'}, dimensions={0}, use_global_device_ids=true | all-gather | bytes 24 | tf_op jit(solution)/shard_map/all_gather | solution.py:23
  20.5 2.5 all-reduce
  23.0 13.7 %all-gather.5 = f32[8,1,2]{2,1,0:T(1,128)S(1)} all-gather(f32[1,1,2]{2,1,0:T(1,128)S(1)} %get-tuple-element.58), channel_id=1, replica_groups=mesh['seq_0'=4,'seq_1'=8,'seq_2'=2,'head'=4] {'seq_1'}, dimensions={0}, use_global_device_ids=true | all-gather | bytes 72 | tf_op jit(solution)/shard_map/all_gather | solution.py:23
  36.7 9.8 %all-gather.3 = f32[8,1,2]{2,1,0:T(1,128)S(1)} all-gather(f32[1,1,2]{2,1,0:T(1,128)S(1)} %get-tuple-element.59), channel_id=1, replica_groups=mesh['seq_0'=4,'seq_1'=8,'seq_2'=2,'head'=4] {'seq_1'}, dimensions={0}, use_global_device_ids=true | all-gather | bytes 72 | tf_op jit(solution)/shard_map/all_gather | solution.py:23
  46.5 8.0 %all-gather.6 = f32[4,1,2]{2,1,0:T(1,128)S(1)} all-gather(f32[1,1,2]{2,1,0:T(1,128)S(1)} %fusion.188), channel_id=1, replica_groups=mesh['seq_0'=4,'seq_1'=8,'seq_2'=2,'head'=4] {'seq_0'}, dimensions={0}, use_global_device_ids=true | all-gather | bytes 40 | tf_op jit(solution)/shard_map/all_gather | solution.py:23
  54.5 5.2 %all-gather.4 = f32[4,1,2]{2,1,0:T(1,128)S(1)} all-gather(f32[1,1,2]{2,1,0:T(1,128)S(1)} %fusion.198), channel_id=1, replica_groups=mesh['seq_0'=4,'seq_1'=8,'seq_2'=2,'head'=4] {'seq_0'}, dimensions={0}, use_global_device_ids=true | all-gather | bytes 40 | tf_op jit(solution)/shard_map/all_gather | solution.py:23
  59.9 2.8 fusion.29
  62.8 102.6 %all-gather.11.cloned.1.call-done = f32[8,2,512,256]{3,2,1,0:T(8,128)} async-done(((f32[1,2,512,256]{3,2,1,0:T(8,128)}), f32[8,2,512,256]{3,2,1,0:T(8,128)}) %all-gather.11.cloned.1.call-update) | async-done | bytes 8388624 | tf_op jit(solution)/shard_map/all_gather | solution.py:23
  165.4 5.3 %multiply_add_fusion = f32[1,2,512,256]{3,2,1,0:T(8,128)} fusion(f32[8,2,512,256]{3,2,1,0:T(8,128)} %all-gather.11.cloned.1.call-done, f32[2]{0:T(128)S(1)} %get-tuple-element.26, f32[2]{0:T(128)S(1)} %get-tuple-element.37, f32[2]{0:T(128)S(1)} %get-tuple-element.34, f32[2]{0:T(128)S(1)} %get-tuple-element.41, f32[2]{0:T(128)S(1)} %get-tuple-element.40, ...), kind=kLoop, calls=%fused_computation.81 | loop fusion | flops 6029312 | bytes 9437312 | tf_op jit(solution)/shard_map/add | solution.py:49
  170.7 1.0 copy.61
  172.2 1.3 multiply_reduce_fusion
  173.5 2.3 all_gather.65
  175.9 16.8 %all_gather.66 = f32[8,2,256]{2,1,0:T(2,128)S(1)} all-gather(f32[1,2,256]{2,1,0:T(2,128)S(1)} %multiply_add_fusion.2), channel_id=1, replica_groups=mesh['seq_0'=4,'seq_1'=8,'seq_2'=2,'head'=4] {'seq_1'}, dimensions={0}, use_global_device_ids=true | all-gather | bytes 18432 | tf_op jit(solution)/shard_map/all_gather | solution.py:23
  192.8 9.8 %all_gather.67 = f32[4,2,256]{2,1,0:T(2,128)S(1)} all-gather(f32[1,2,256]{2,1,0:T(2,128)S(1)} %multiply_add_fusion.1), channel_id=1, replica_groups=mesh['seq_0'=4,'seq_1'=8,'seq_2'=2,'head'=4] {'seq_0'}, dimensions={0}, use_global_device_ids=true | all-gather | bytes 10240 | tf_op jit(solution)/shard_map/all_gather | solution.py:23
  203.6 1.1 fusion.218
  204.8 2.0 fusion.72
  206.9 13.5 %all-gather.13.cloned.1.call-done = f32[4,2,512,256]{3,2,1,0:T(8,128)} async-done(((f32[1,2,512,256]{3,2,1,0:T(8,128)}), f32[4,2,512,256]{3,2,1,0:T(8,128)}) %all-gather.13.cloned.1.call-update) | async-done | bytes 4194320 | tf_op jit(solution)/shard_map/all_gather | solution.py:23
  220.3 8.7 %fusion.2 = bf16[512,2,512]{0,2,1:T(8,128)(2,1)S(1)} fusion(f32[2,512,512]{1,2,0:T(8,128)} %fusion.72, bf16[512,2,256]{0,2,1:T(8,128)(2,1)} %bitcast.668, f32[4,2,512,256]{3,2,1,0:T(8,128)} %all-gather.13.cloned.1.call-done, f32[512,2]{0,1:T(2,128)S(1)} %get-tuple-element.2, f32[512,2]{0,1:T(2,128)S(1)} %get-tuple-element.4, ...), kind=kOutput, calls=%fused_computation.4 | convolution fusion | flops 1629224960 | bytes 18362654 | tf_op jit(solution)/shard_map/hvk,thk->thv/dot_general | solution.py:98
  229.0 9.5 %convolution_convert_fusion = bf16[512,4096]{1,0:T(8,128)(2,1)} fusion(bf16[512,1024]{0,1:T(8,128)(2,1)S(1)} %bitcast.678, bf16[1024,4096]{1,0:T(8,128)(2,1)} %param.11), kind=kOutput, calls=%fused_computation | convolution fusion | flops 4297064448 | bytes 13631488 | tf_op jit(solution)/shard_map/dot_general | solution.py:126
  238.6 18.9 %all_to_all.6 = f32[64,1,2]{2,1,0:T(1,128)S(1)} all-to-all(f32[64,1,2]{2,1,0:T(1,128)S(1)} %broadcast_in_dim.18), channel_id=1, replica_groups=mesh['seq_0'=4,'seq_1'=8,'seq_2'=2,'head'=4] {'seq_0','seq_1','seq_2'}, dimensions={0} | all-to-all | bytes 1024 | tf_op jit(solution)/shard_map/all_to_all | solution.py:35
  258.1 30.3 %reduce-scatter.2.cloned.1.call-done = bf16[512,1024]{1,0:T(8,128)(2,1)} async-done(((bf16[512,4096]{1,0:T(8,128)(2,1)}), bf16[512,1024]{1,0:T(8,128)(2,1)}) %reduce-scatter.2.cloned.1.call-update) | async-done | bytes 1048592 | tf_op jit(solution)/shard_map/reduce_scatter | solution.py:127
  (60 shorter events, 6.4 us)
Async XLA Ops:
  7.2 5.0 %copy-start.5 = (f32[512,2]{0,1:T(2,128)S(1)}, f32[512,2]{0,1:T(2,128)}, u32[]{:S(2)}) copy-start(f32[512,2]{0,1:T(2,128)} %param.10) | copy-start | bytes 12292
  7.2 52.7 %all-gather.15.cloned.1.call-start = ((), (), s32[]{:S(2)}) async-start(), calls=%async_computation.5 | async-start | bytes 3145728 | tf_op jit(solution)/shard_map/all_gather | solution.py:23
  10.4 2.5 copy-start
  12.9 1.4 copy-start.6
  14.3 151.1 %all-gather.11.cloned.1.call-start = ((), (), s32[]{:S(2)}) async-start(), calls=%async_computation.2 | async-start | bytes 9437184 | tf_op jit(solution)/shard_map/all_gather | solution.py:23
  62.7 157.6 %all-gather.13.cloned.1.call-start = ((), (), s32[]{:S(2)}) async-start(), calls=%async_computation.3 | async-start | bytes 5242880 | tf_op jit(solution)/shard_map/all_gather | solution.py:23
  165.4 5.4 %copy-start.4 = (bf16[512,512]{1,0:T(8,128)(2,1)S(1)}, bf16[512,512]{1,0:T(8,128)(2,1)}, u32[]{:S(2)}) copy-start(bf16[512,512]{1,0:T(8,128)(2,1)} %param.6) | copy-start | bytes 1572868
  170.7 117.7 %reduce-scatter.2.cloned.1.call-start = ((), (), s32[]{:S(2)}) async-start(), calls=%async_computation.4 | async-start | bytes 5242880 | tf_op jit(solution)/shard_map/reduce_scatter | solution.py:127
  172.2 31.1 %copy-start.3 = (bf16[512,512]{0,1:T(8,128)(2,1)S(1)}, bf16[512,512]{0,1:T(8,128)(2,1)}, u32[]{:S(2)}) copy-start(bf16[512,512]{0,1:T(8,128)(2,1)} %copy.61) | copy-start | bytes 1572868
  172.2 31.4 %copy-start.1 = (bf16[512,512]{0,1:T(8,128)(2,1)S(1)}, bf16[512,512]{0,1:T(8,128)(2,1)}, u32[]{:S(2)}) copy-start(bf16[512,512]{0,1:T(8,128)(2,1)} %copy-done) | copy-start | bytes 1572868
  204.8 15.5 %copy-start.2 = (f32[4,512,256]{2,1,0:T(8,128)S(1)}, f32[4,512,256]{2,1,0:T(8,128)}, u32[]{:S(2)}) copy-start(f32[4,512,256]{2,1,0:T(8,128)} %all-gather.15.cloned.1.call-done) | copy-start | bytes 6291460
Sparse Core Ops, SparseCore 0:
  14.4 20.3 all-gather.14
  62.8 102.5 all-gather.10
  170.8 49.4 all-gather.12
  238.7 49.6 reduce-scatter.1
where the time goes:
time: 295 us
  waiting for transfers between devices  146 us (49%)
  blocking collectives  91.6 us (31%)
  matrix products  22.1 us (7%)
  between operations  14.7 us (5%)
  other arithmetic  13 us (4%)
  local copies, waits for them, and re-layouts  6.97 us (2%)
    all_gather x3, waiting for transfers between devices, entering(): pieces = jax.tree.map(lambda part: lax.all_gather(part, axis), so_far)  116 us
    all_gather x8, blocking collectives, entering(): pieces = jax.tree.map(lambda part: lax.all_gather(part, axis), so_far)  70.3 us
    reduce_scatter x1, waiting for transfers between devices, shards(): lax.psum_scatter(partial_value.astype(jnp.bfloat16), 'head', scatter_dime...  30.3 us
    all_to_all x1, blocking collectives, copy_for_each(): return lax.all_to_all(copies, axis, split_axis=0, concat_axis=0, tiled=True)  18.9 us
    dot_general x1, matrix products, shards(): jnp.dot(hidden, out_weight, preferred_element_type=jnp.float32)  9.48 us
    dot_general x1, matrix products, readout(): jnp.einsum('hvk,thk->thv', carry_matrix, q_float, precision=lax.Precision...  8.7 us
    add x2, other arithmetic, combine_states(): e_scale[:, None, None] * e_matrix + l_scale[:, None, None] * l_matrix  8.04 us
  transfers between devices with their start and end apart: 4, of which 3 were waited for; matrix products, arithmetic and copies ran while one was open for 3% of the time, Pallas kernels for 0%

commit v1 on v0

v1 whole, which is shorter than its diff:
```python
import functools

import jax
import jax.numpy as jnp
from jax import lax
from jax.experimental import pallas as pl
from jax.experimental.pallas import tpu as pltpu
from jax.sharding import Mesh
from jax.sharding import PartitionSpec as P

MESH = pl.DeviceIdType.MESH
SEQ = ("y", "z", "c")
F32 = jnp.float32
BF16 = jnp.bfloat16
LOW = -1e30
INFO = 640


def dot(a, b):
    return jnp.dot(a, b, preferred_element_type=F32)


def merge(e_max, l_max, l_decay):
    top = jnp.maximum(l_decay + e_max, l_max)
    return jnp.exp(l_decay + e_max - top), jnp.exp(l_max - top), top


def three_rows(row, first):
    hi = row.astype(BF16).astype(F32)
    mid = (row - hi).astype(BF16).astype(F32)
    low = row - hi - mid
    return jnp.where(first == 0, hi, jnp.where(first == 1, mid, jnp.where(first == 2, low, 0.0))).astype(BF16)


def read_info(ref, j):
    row = ref[j]
    return row[:, :256], row[:, 256:257], row[:, 384:385], row[:, 512:513]


def write_info(ref, norm, top, decay, gate):
    ref[0, :, 0:256] = norm
    ref[0, :, 256:384] = jnp.broadcast_to(top, (1, 128))
    ref[0, :, 384:512] = jnp.broadcast_to(decay, (1, 128))
    ref[0, :, 512:640] = jnp.broadcast_to(gate, (1, 128))


def kernel(
    sizes,
    q_hbm, k_hbm, v_hbm, fg_hbm, ig_hbm, w_hbm,
    mixed_hbm, gate_ref,
    q_buf, k_buf, v_buf, fg_buf, ig_buf, w_buf, kt_buf,
    own1, pair_out, pair_in, pinfo_out, pinfo_in,
    t_buf, t_in, tinfo_out, tinfo,
    p_buf, y_out, y_in, yinfo_out, yinfo,
    e_buf, e_in, f_out, f_in, finfo_out, finfo_in, mine,
    num_buf, bmax_buf, den_buf, hid,
    s1_out, s1_in, dir_out, dir_in, rel_out, rel_in, own_p, rel_p, out_buf,
    load_sem, w_sem, out_sem,
    pair_ss, pair_rs, z_ss, z_rs, zi_ss, zi_rs, y_ss, y_rs, yi_ss, yi_rs, e_ss, e_rs, f_ss, f_rs,
    s1_ss, s1_rs, dir_ss, dir_rs, rel_ss, rel_rs,
):
    ny, nz, nx = sizes
    y, z, c, x = (lax.axis_index(a) for a in ("y", "z", "c", "x"))
    tokens = q_buf.shape[1]
    dk, dv = q_buf.shape[2], v_buf.shape[2]
    half = tokens // 2
    cols = w_buf.shape[2]
    share = dk // nz
    first = c == 0
    heads = (1 - c, c)

    loads = []

    def load(src, dst):
        copy = pltpu.make_async_copy(src, dst, load_sem.at[len(loads)])
        copy.start()
        loads.append(copy)

    load(fg_hbm, fg_buf)
    load(ig_hbm, ig_buf)
    for s in range(2):
        load(k_hbm.at[:, pl.ds(pl.multiple_of(heads[s] * dk, 128), dk)], k_buf.at[s])
        load(v_hbm.at[:, pl.ds(pl.multiple_of(heads[s] * dv, 128), dv)], v_buf.at[s])
    for s in range(2):
        load(q_hbm.at[:, pl.ds(pl.multiple_of(heads[s] * dk, 128), dk)], q_buf.at[s])

    barrier = pltpu.get_barrier_semaphore()
    peers = [{"c": 1 - c}]
    peers += [{"z": lax.rem(z + d, nz)} for d in range(1, nz)]
    peers += [{"y": lax.rem(y + d, ny)} for d in range(1, ny)]
    left, right = {"x": lax.rem(x + nx - 1, nx)}, {"x": lax.rem(x + 1, nx)}
    peers += [left, right]
    for peer in peers:
        pl.semaphore_signal(barrier, inc=1, device_id=peer, device_id_type=MESH)

    targets = (lax.rem(x + 2, nx), lax.rem(x + nx - 1, nx), lax.rem(x + 1, nx), x)
    w_loads = []
    for i in range(4):
        for s in range(2):
            copy = pltpu.make_async_copy(
                w_hbm.at[pl.ds(pl.multiple_of(heads[s] * dv, 128), dv), pl.ds(pl.multiple_of(targets[i] * cols, 128), cols)],
                w_buf.at[i, pl.ds(s * dv, dv), :],
                w_sem.at[2 * i + s],
            )
            copy.start()
            w_loads.append(copy)

    loads[0].wait()
    loads[1].wait()
    fg, ig = fg_buf[...], ig_buf[...]
    lf = jnp.minimum(fg, 0.0) - jnp.log1p(jnp.exp(-jnp.abs(fg)))
    lf_rows = (jnp.where(first, lf[1:2], lf[0:1]), jnp.where(first, lf[0:1], lf[1:2]))
    ig_rows = (jnp.where(first, ig[1:2], ig[0:1]), jnp.where(first, ig[0:1], ig[1:2]))
    sub = lax.broadcasted_iota(jnp.int32, (8, tokens), 0)
    upper = (
        lax.broadcasted_iota(jnp.int32, (tokens, tokens), 0) <= lax.broadcasted_iota(jnp.int32, (tokens, tokens), 1)
    ).astype(F32).astype(BF16)
    stacked = jnp.where(
        sub < 4,
        three_rows(jnp.broadcast_to(lf_rows[0], (8, tokens)), sub).astype(F32),
        three_rows(jnp.broadcast_to(lf_rows[1], (8, tokens)), sub - 4).astype(F32),
    ).astype(BF16)
    cums = dot(stacked, upper)
    b_rows, decays, tops, weights = [], [], [], []
    for s in range(2):
        cum = jnp.sum(cums[4 * s : 4 * s + 4], axis=0, keepdims=True)
        b = ig_rows[s] - cum
        decay = cum[:, tokens - 1 : tokens]
        b_top = jnp.max(b, axis=1, keepdims=True)
        b_rows.append(b)
        decays.append(decay)
        tops.append(decay + b_top)
        weights.append(jnp.exp(b - b_top) * (dk**-0.5))
    gates = [jnp.sum(ig_rows[s], axis=1, keepdims=True) for s in range(2)]

    def own_state(s):
        kt = k_buf[s].T
        kt_buf[s] = kt
        wkt = (kt.astype(F32) * weights[s]).astype(BF16)
        matrix = dot(wkt, v_buf[s])
        norm = jnp.sum(dot(three_rows(jnp.broadcast_to(weights[s], (8, tokens)), sub), k_buf[s]), axis=0, keepdims=True)
        return matrix, norm

    def remote(src, dst, ss, rs, peer):
        return pltpu.make_async_remote_copy(
            src_ref=src, dst_ref=dst, send_sem=ss, recv_sem=rs, device_id=peer, device_id_type=MESH
        )

    sends = []

    loads[2].wait()
    loads[3].wait()
    matrix0, norm0 = own_state(0)
    pair_out[...] = matrix0.astype(BF16)
    write_info(pinfo_out, norm0, tops[0], decays[0], gates[0])
    pl.semaphore_wait(barrier, len(peers))
    partner = {"c": 1 - c}
    pair = [
        remote(pinfo_out, pinfo_in, pair_ss.at[0], pair_rs.at[0], partner),
        remote(pair_out, pair_in, pair_ss.at[1], pair_rs.at[1], partner),
    ]
    for copy in pair:
        copy.start()
    sends += pair

    loads[4].wait()
    loads[5].wait()
    matrix1, norm1 = own_state(1)
    own1[...] = matrix1

    pair[0].wait_recv()
    in_norm, in_top, in_decay, in_gate = read_info(pinfo_in, 0)
    a_top, a_norm = jnp.where(first, tops[1], in_top), jnp.where(first, norm1, in_norm)
    a_decay = jnp.where(first, decays[1], in_decay)
    l_top, l_norm = jnp.where(first, in_top, tops[1]), jnp.where(first, in_norm, norm1)
    l_decay = jnp.where(first, in_decay, decays[1])
    e_scale, l_scale, chip_top = merge(a_top, l_top, l_decay)
    chip_norm = e_scale * a_norm + l_scale * l_norm
    write_info(tinfo_out, chip_norm, chip_top, a_decay + l_decay, gates[1] + in_gate)
    zi = []
    order = sorted(range(1, nz), key=lambda d: -min(d, nz - d))
    for d in order:
        copy = remote(tinfo_out.at[0], tinfo.at[z], zi_ss.at[d], zi_rs.at[d], {"z": lax.rem(z + d, nz)})
        copy.start()
        zi.append(copy)
    tinfo[z] = tinfo_out[0]
    own_scale, in_scale = jnp.where(first, e_scale, l_scale), jnp.where(first, l_scale, e_scale)
    pair[1].wait_recv()
    zs = []
    for j in range(nz):
        rows = pl.ds(j * share, share)
        t_buf[j] = (own_scale * own1[rows, :] + in_scale * pair_in[rows, :].astype(F32)).astype(BF16)
    for d in order:
        peer = lax.rem(z + d, nz)
        copy = remote(t_buf.at[peer], t_in.at[z], z_ss.at[d], z_rs.at[d], {"z": peer})
        copy.start()
        zs.append(copy)
    t_in[z] = t_buf[z]
    sends += zi + zs

    loads[6].wait()
    loads[7].wait()

    def intra(s):
        for r in range(2):
            rows = pl.ds(r * half, half)
            span = half * (r + 1)
            scores = dot(q_buf[s, rows, :], kt_buf[s, :, :span]) * (dk**-0.5)
            t_index = lax.broadcasted_iota(jnp.int32, (half, span), 0) + r * half
            s_index = lax.broadcasted_iota(jnp.int32, (half, span), 1)
            logs = jnp.where(s_index <= t_index, jnp.broadcast_to(b_rows[s][:, :span], (half, span)), -jnp.inf)
            top = jnp.max(logs, axis=1, keepdims=True)
            weighted = jnp.exp(logs - top) * scores
            bmax_buf[s, rows, :] = top
            den_buf[s, rows, :] = jnp.sum(weighted, axis=1, keepdims=True)
            num_buf[s, rows, :] = dot(weighted.astype(BF16), v_buf[s, :span, :])

    intra(1)
    intra(0)

    for copy in zi:
        copy.wait_recv()
    top, decay, norm, gate = jnp.full((1, 1), LOW, F32), jnp.zeros((1, 1), F32), jnp.zeros((1, dk), F32), jnp.zeros((1, 1), F32)
    z_norm, z_top, z_decay = norm, top, decay
    z_tops, z_decays, scales = [], [], []
    for j in range(nz):
        z_tops.append(top)
        z_decays.append(decay)
        here = j == z
        z_norm, z_top, z_decay = jnp.where(here, norm, z_norm), jnp.where(here, top, z_top), jnp.where(here, decay, z_decay)
        j_norm, j_top, j_decay, j_gate = read_info(tinfo, j)
        e_scale, l_scale, top = merge(top, j_top, j_decay)
        norm = e_scale * norm + l_scale * j_norm
        decay = decay + j_decay
        gate = gate + j_gate
        scales.append((e_scale, l_scale))
    write_info(yinfo_out, norm, top, decay, gate)
    yi = []
    y_order = sorted(range(1, ny), key=lambda d: -min(d, ny - d))
    for d in y_order:
        copy = remote(yinfo_out.at[0], yinfo.at[y], yi_ss.at[d], yi_rs.at[d], {"y": lax.rem(y + d, ny)})
        copy.start()
        yi.append(copy)
    yinfo[y] = yinfo_out[0]
    for copy in zs:
        copy.wait_recv()
    running = jnp.zeros((share, dv), F32)
    for j in range(nz):
        p_buf[j] = running
        running = scales[j][0] * running + scales[j][1] * t_in[j].astype(F32)
    y_out[...] = running.astype(BF16)
    ys = []
    for d in y_order:
        copy = remote(y_out, y_in.at[y], y_ss.at[d], y_rs.at[d], {"y": lax.rem(y + d, ny)})
        copy.start()
        ys.append(copy)
    y_in[y] = y_out[...]
    sends += yi + ys

    for copy in yi:
        copy.wait_recv()
    top, decay, norm, gate = jnp.full((1, 1), LOW, F32), jnp.zeros((1, 1), F32), jnp.zeros((1, dk), F32), jnp.zeros((1, 1), F32)
    y_scales = []
    for j in range(ny):
        j_norm, j_top, j_decay, j_gate = read_info(yinfo, j)
        passed = j < y
        e_scale, l_scale, next_top = merge(top, j_top, j_decay)
        norm = jnp.where(passed, e_scale * norm + l_scale * j_norm, norm)
        top = jnp.where(passed, next_top, top)
        gate = gate + j_gate
        y_scales.append((jnp.where(passed, e_scale, 1.0), jnp.where(passed, l_scale, 0.0)))
    e_scales = [merge(top, z_tops[j], z_decays[j]) for j in range(nz)]
    e_scale, l_scale, chip_max = merge(top, z_top, z_decay)
    enter_norm = e_scale * norm + l_scale * z_norm
    for copy in ys:
        copy.wait_recv()
    before = jnp.zeros((share, dv), F32)
    for j in range(ny):
        before = y_scales[j][0] * before + y_scales[j][1] * y_in[j].astype(F32)
    for j in range(nz):
        e_buf[j] = (e_scales[j][0] * before + e_scales[j][1] * p_buf[j]).astype(BF16)
    es = []
    for d in order:
        peer = lax.rem(z + d, nz)
        copy = remote(e_buf.at[peer], e_in.at[z], e_ss.at[d], e_rs.at[d], {"z": peer})
        copy.start()
        es.append(copy)
    e_in[z] = e_buf[z]
    sends += es

    e_scale, l_scale, both_max = merge(chip_max, a_top, a_decay)
    both_norm = e_scale * enter_norm + l_scale * a_norm
    my_max, my_norm = jnp.where(first, chip_max, both_max), jnp.where(first, enter_norm, both_norm)
    write_info(finfo_out, jnp.where(first, both_norm, enter_norm), jnp.where(first, both_max, chip_max), a_decay, gate)
    finish = [remote(finfo_out, finfo_in, f_ss.at[0], f_rs.at[0], partner), remote(f_out, f_in, f_ss.at[1], f_rs.at[1], partner)]
    finish[0].start()
    for copy in es:
        copy.wait_recv()
    for j in range(nz):
        rows = pl.ds(j * share, share)
        entering = e_in[j].astype(F32)
        a_rows = jnp.where(first, own1[rows, :], pair_in[rows, :].astype(F32))
        both = e_scale * entering + l_scale * a_rows
        f_out[rows, :] = jnp.where(first, both, entering).astype(BF16)
        mine[rows, :] = jnp.where(first, entering, both).astype(BF16)
    finish[1].start()
    sends += finish

    def readout(s, carry, norm, top):
        for r in range(2):
            rows = pl.ds(r * half, half)
            q = q_buf[s, rows, :]
            carried = dot(q, carry[...])
            carried_den = jnp.sum(q.astype(F32) * norm, axis=1, keepdims=True)
            b_top = bmax_buf[s, rows, :]
            stabilizer = jnp.maximum(b_top, top)
            a, k = jnp.exp(b_top - stabilizer), jnp.exp(top - stabilizer)
            den = a * den_buf[s, rows, :] + k * carried_den
            inverse = 1.0 / jnp.maximum(jnp.abs(den), 1.0)
            hid[rows, s * dv : (s + 1) * dv] = ((a * inverse) * num_buf[s, rows, :] + (k * inverse) * carried).astype(BF16)

    readout(1, mine, my_norm, my_max)
    finish[0].wait_recv()
    other_norm, other_max, unused_decay, other_gate = read_info(finfo_in, 0)
    scale = 1.0 / (tokens * ny * nz * 2)
    kept, got = (gate * scale)[0, 0], (other_gate * scale)[0, 0]
    gate_ref[0] = jnp.where(first, kept, got)
    gate_ref[1] = jnp.where(first, got, kept)
    finish[1].wait_recv()
    readout(0, f_in, other_norm, other_max)

    step = 256
    quarter = tokens // 4

    def project(i, part, store):
        def body(n, carry):
            at = pl.ds(pl.multiple_of(n * step, step), step)
            out = dot(hid[part * half : (part + 1) * half, :], w_buf[i, :, at])
            store(part, at, out)
            return carry

        lax.fori_loop(0, cols // step, body, 0)

    def to(buf):
        def store(part, at, out):
            for r in range(2):
                buf[2 * part + r, :, at] = out[r * quarter : (r + 1) * quarter].astype(buf.dtype)

        return store

    def ship(src, dst, ss, rs, r, peer):
        copy = remote(src.at[r], dst.at[r], ss.at[r], rs.at[r], peer)
        copy.start()
        return copy

    for i in range(2):
        w_loads[i].wait()
    stage1 = [None] * 4
    for part in range(2):
        project(0, part, to(s1_out))
        for r in (2 * part, 2 * part + 1):
            stage1[r] = ship(s1_out, s1_in, s1_ss, s1_rs, r, left if part == 0 else right)
    direct = [None] * 4
    for i, part, peer in ((1, 1, left), (2, 0, right)):
        w_loads[2 * i].wait()
        w_loads[2 * i + 1].wait()
        project(i, part, to(dir_out))
        for r in (2 * part, 2 * part + 1):
            direct[r] = ship(dir_out, dir_in, dir_ss, dir_rs, r, peer)
    project(1, 0, to(rel_p))
    project(2, 1, to(rel_p))
    relay = [None] * 4
    for r in (0, 2, 1, 3):
        if r == 1:
            w_loads[6].wait()
            w_loads[7].wait()
            project(3, 0, to(own_p))
            project(3, 1, to(own_p))
        stage1[r].wait_recv()
        rel_out[r] = (rel_p[r] + s1_in[r].astype(F32)).astype(BF16)
        relay[r] = ship(rel_out, rel_in, rel_ss, rel_rs, r, left if r < 2 else right)
    sends += stage1 + direct + relay
    outs = []
    for r in (0, 2, 1, 3):
        direct[r].wait_recv()
        relay[r].wait_recv()
        out_buf[r] = (own_p[r] + dir_in[r].astype(F32) + rel_in[r].astype(F32)).astype(BF16)
        copy = pltpu.make_async_copy(out_buf.at[r], mixed_hbm.at[pl.ds(r * quarter, quarter), :], out_sem.at[r])
        copy.start()
        outs.append(copy)
    for copy in sends:
        copy.wait_send()
    for copy in outs:
        copy.wait()


def shards(queries, keys, values, forget_gate, input_gate, out_weight):
    tokens, heads = forget_gate.shape
    dk, dv = queries.shape[1] // heads, values.shape[1] // heads
    width = out_weight.shape[1]
    ny, nz, nx = (lax.axis_size(a) for a in ("y", "z", "x"))
    cols = width // nx
    share = dk // nz
    quarter = tokens // 4
    any_space = pl.BlockSpec(memory_space=pl.ANY)
    dma = pltpu.SemaphoreType.DMA
    info = lambda n: pltpu.VMEM((n, 1, INFO), F32)
    quad = lambda kind: pltpu.VMEM((4, quarter, cols), kind)
    mixed, gate_mean = pl.pallas_call(
        functools.partial(kernel, (ny, nz, nx)),
        out_shape=(jax.ShapeDtypeStruct((tokens, cols), BF16), jax.ShapeDtypeStruct((heads,), F32)),
        in_specs=[any_space] * 6,
        out_specs=(any_space, pl.BlockSpec(memory_space=pltpu.SMEM)),
        scratch_shapes=[
            pltpu.VMEM((2, tokens, dk), BF16),
            pltpu.VMEM((2, tokens, dk), BF16),
            pltpu.VMEM((2, tokens, dv), BF16),
            pltpu.VMEM((heads, tokens), F32),
            pltpu.VMEM((heads, tokens), F32),
            pltpu.VMEM((4, heads * dv, cols), BF16),
            pltpu.VMEM((2, dk, tokens), BF16),
            pltpu.VMEM((dk, dv), F32),
            pltpu.VMEM((dk, dv), BF16),
            pltpu.VMEM((dk, dv), BF16),
            info(1),
            info(1),
            pltpu.VMEM((nz, share, dv), BF16),
            pltpu.VMEM((nz, share, dv), BF16),
            info(1),
            info(nz),
            pltpu.VMEM((nz, share, dv), F32),
            pltpu.VMEM((share, dv), BF16),
            pltpu.VMEM((ny, share, dv), BF16),
            info(1),
            info(ny),
            pltpu.VMEM((nz, share, dv), BF16),
            pltpu.VMEM((nz, share, dv), BF16),
            pltpu.VMEM((dk, dv), BF16),
            pltpu.VMEM((dk, dv), BF16),
            info(1),
            info(1),
            pltpu.VMEM((dk, dv), BF16),
            pltpu.VMEM((2, tokens, dv), F32),
            pltpu.VMEM((2, tokens, 1), F32),
            pltpu.VMEM((2, tokens, 1), F32),
            pltpu.VMEM((tokens, heads * dv), BF16),
            quad(BF16), quad(BF16), quad(BF16), quad(BF16), quad(BF16), quad(BF16),
            quad(F32), quad(F32), quad(BF16),
            dma((8,)), dma((8,)), dma((4,)),
            dma((2,)), dma((2,)),
            dma((nz,)), dma((nz,)), dma((nz,)), dma((nz,)),
            dma((ny,)), dma((ny,)), dma((ny,)), dma((ny,)),
            dma((nz,)), dma((nz,)),
            dma((2,)), dma((2,)),
            dma((4,)), dma((4,)), dma((4,)), dma((4,)), dma((4,)), dma((4,)),
        ],
        compiler_params=pltpu.CompilerParams(
            collective_id=0, has_side_effects=True, vmem_limit_bytes=60 * 1024 * 1024
        ),
        name="mlstm_layer",
    )(queries, keys, values, forget_gate.T, input_gate.T, out_weight)
    return mixed, gate_mean


def solution(mesh):
    torus = Mesh(mesh.devices.reshape(4, 8, 2, mesh.shape["head"]), ("y", "z", "c", "x"))
    both = P(SEQ, "x")
    return jax.shard_map(
        shards,
        mesh=torus,
        in_specs=(both, both, both, both, both, P("x", None)),
        out_specs=(P(SEQ, "x"), P("x")),
        check_vma=False,
    )
```

time: 295 us -> 79.3 us (0.27)
  waiting for transfers between devices: 146 us -> 0 us
  blocking collectives: 91.6 us -> 0 us
  Pallas kernels: 0 us -> 75.1 us
  matrix products: 22.1 us -> 0 us
  between operations: 14.7 us -> 0.64 us
  other arithmetic: 13 us -> 0 us
  local copies, waits for them, and re-layouts: 6.97 us -> 3.38 us
    all_gather x3 -> x0, waiting for transfers between devices: 116 us -> none  [entering(): pieces = jax.tree.map(lambda part: lax.all_gather(part, axis), so_far)]
    pallas_call x0 -> x1, Pallas kernels: none -> 75.1 us  [shards(): pl.pallas_call(functools.partial(kernel, (ny, nz, nx)), out_shape=(jax.Sh...]
    all_gather x8 -> x0, blocking collectives: 70.3 us -> none  [entering(): pieces = jax.tree.map(lambda part: lax.all_gather(part, axis), so_far)]
    reduce_scatter x1 -> x0, waiting for transfers between devices: 30.3 us -> none  [shards(): lax.psum_scatter(partial_value.astype(jnp.bfloat16), 'head', scatter_dime...]
    dot_general x6 -> x0, matrix products: 22.1 us -> none  [the longest x1 9.48 us: shards(): jnp.dot(hidden, out_weight, preferred_element_type=jnp.float32)]
    all_to_all x1 -> x0, blocking collectives: 18.9 us -> none  [copy_for_each(): return lax.all_to_all(copies, axis, split_axis=0, concat_axis=0, tiled=True)]
    add x6 -> x0, other arithmetic: 8.36 us -> none  [the longest x2 8.04 us: combine_states(): e_scale[:, None, None] * e_matrix + l_scale[:, None, None] * l_matrix]
    reshape x4 -> x0, local copies, waits for them, and re-layouts: 3.96 us -> none  [the longest x1 1.69 us: shards(): v_heads = values.reshape(token_count, head_count, v_width)]
  transfers between devices with their start and end apart: 4 -> 0, of which waited for: 3 -> 0; matrix products, arithmetic and copies ran while one was open for 3% -> 0% of each run, Pallas kernels for 0% -> 0%
where the time goes in v1:
time: 79.3 us; the launch traced here: 79.1 us
  Pallas kernels  75.1 us (95%)
  local copies, waits for them, and re-layouts  3.38 us (4%)
    pallas_call x1, Pallas kernels, shards(): pl.pallas_call(functools.partial(kernel, (ny, nz, nx)), out_shape=(jax.Sh...  75.1 us
    unnamed x2, local copies, waits for them, and re-layouts  3.38 us

profile of v1, /device:TPU:1, one launch (start us, length us, event | category | flops | bytes accessed | tf_op | source)
XLA Modules:
  0.0 79.1 jit_solution(14099420885740043797)
XLA Ops:
  0.6 75.1 %mlstm_layer.1 = (bf16[512,1024]{1,0:T(8,128)(2,1)}, f32[2]{0:T(128)}) custom-call(bf16[512,512]{1,0:T(8,128)(2,1)} %q_hbm.1, bf16[512,512]{1,0:T(8,128)(2,1)} %k_hbm.1, bf16[512,1024]{1,0:T(8,128)(2,1)} %v_hbm.1, f32[2,512]{1,0:T(2,128)} %bitcast.2, f32[2,512]{1,0:T(2,128)} %bitcast.3, bf16[1024,4096]{1,0:T(8,128)(2,1)} %w_hbm.1), custom_call_target="tpu_custom_call" | custom-call | tf_op jit(solution)/shard_map/mlstm_layer/pallas_call | solution.py:409
  75.8 2.3 %copy.10 = bf16[512,1024]{1,0:T(8,128)(2,1)} copy(bf16[512,1024]{1,0:T(8,128)(2,1)} %get-tuple-element.4) | data formatting | bytes 2097152
  78.0 1.1 %copy.11 = f32[2]{0:T(128)} copy(f32[2]{0:T(128)} %get-tuple-element.5) | data formatting | bytes 16

commit v2 on v1

--- a/solution.py
+++ b/solution.py
@@ -47,16 +47,16 @@
 def kernel(
     sizes,
     q_hbm, k_hbm, v_hbm, fg_hbm, ig_hbm, w_hbm,
-    mixed_hbm, gate_ref,
+    mixed_ref, gate_ref,
     q_buf, k_buf, v_buf, fg_buf, ig_buf, w_buf, kt_buf,
     own1, pair_out, pair_in, pinfo_out, pinfo_in,
     t_buf, t_in, tinfo_out, tinfo,
     p_buf, y_out, y_in, yinfo_out, yinfo,
     e_buf, e_in, f_out, f_in, finfo_out, finfo_in, mine,
     num_buf, bmax_buf, den_buf, hid,
-    s1_out, s1_in, dir_out, dir_in, rel_out, rel_in, own_p, rel_p, out_buf,
-    load_sem, w_sem, out_sem,
-    pair_ss, pair_rs, z_ss, z_rs, zi_ss, zi_rs, y_ss, y_rs, yi_ss, yi_rs, e_ss, e_rs, f_ss, f_rs,
+    s1_out, s1_in, dir_out, dir_in, rel_out, rel_in, own_p,
+    load_sem, w_sem,
+    pair_ss, pair_rs, z_ss, z_rs, zi_ss, zi_rs, y_ss, y_rs, yi_ss, yi_rs, e_ss, e_rs, f_ss, f_rs, fi_ss, fi_rs,
     s1_ss, s1_rs, dir_ss, dir_rs, rel_ss, rel_rs,
 ):
     ny, nz, nx = sizes
@@ -66,6 +66,7 @@
     half = tokens // 2
     cols = w_buf.shape[2]
     share = dk // nz
+    chunks, wide, step = t_buf.shape[0], t_buf.shape[3], own_p.shape[2]
     first = c == 0
     heads = (1 - c, c)
 
@@ -187,16 +188,20 @@
     own_scale, in_scale = jnp.where(first, e_scale, l_scale), jnp.where(first, l_scale, e_scale)
     pair[1].wait_recv()
     zs = []
-    for j in range(nz):
-        rows = pl.ds(j * share, share)
-        t_buf[j] = (own_scale * own1[rows, :] + in_scale * pair_in[rows, :].astype(F32)).astype(BF16)
-    for d in order:
-        peer = lax.rem(z + d, nz)
-        copy = remote(t_buf.at[peer], t_in.at[z], z_ss.at[d], z_rs.at[d], {"z": peer})
-        copy.start()
-        zs.append(copy)
-    t_in[z] = t_buf[z]
-    sends += zi + zs
+    for h in range(chunks):
+        at = pl.ds(h * wide, wide)
+        for j in range(nz):
+            rows = pl.ds(j * share, share)
+            t_buf[h, j] = (own_scale * own1[rows, at] + in_scale * pair_in[rows, at].astype(F32)).astype(BF16)
+        zs.append([])
+        for d in order:
+            peer = lax.rem(z + d, nz)
+            copy = remote(t_buf.at[h, peer], t_in.at[h, z], z_ss.at[h, d], z_rs.at[h, d], {"z": peer})
+            copy.start()
+            zs[h].append(copy)
+        t_in[h, z] = t_buf[h, z]
+        sends += zs[h]
+    sends += zi
 
     loads[6].wait()
     loads[7].wait()
@@ -242,20 +247,23 @@
         copy.start()
         yi.append(copy)
     yinfo[y] = yinfo_out[0]
-    for copy in zs:
-        copy.wait_recv()
-    running = jnp.zeros((share, dv), F32)
-    for j in range(nz):
-        p_buf[j] = running
-        running = scales[j][0] * running + scales[j][1] * t_in[j].astype(F32)
-    y_out[...] = running.astype(BF16)
     ys = []
-    for d in y_order:
-        copy = remote(y_out, y_in.at[y], y_ss.at[d], y_rs.at[d], {"y": lax.rem(y + d, ny)})
-        copy.start()
-        ys.append(copy)
-    y_in[y] = y_out[...]
-    sends += yi + ys
+    for h in range(chunks):
+        for copy in zs[h]:
+            copy.wait_recv()
+        running = jnp.zeros((share, wide), F32)
+        for j in range(nz):
+            p_buf[h, j] = running
+            running = scales[j][0] * running + scales[j][1] * t_in[h, j].astype(F32)
+        y_out[h] = running.astype(BF16)
+        ys.append([])
+        for d in y_order:
+            copy = remote(y_out.at[h], y_in.at[h, y], y_ss.at[h, d], y_rs.at[h, d], {"y": lax.rem(y + d, ny)})
+            copy.start()
+            ys[h].append(copy)
+        y_in[h, y] = y_out[h]
+        sends += ys[h]
+    sends += yi
 
     for copy in yi:
         copy.wait_recv()
@@ -272,126 +280,130 @@
     e_scales = [merge(top, z_tops[j], z_decays[j]) for j in range(nz)]
     e_scale, l_scale, chip_max = merge(top, z_top, z_decay)
     enter_norm = e_scale * norm + l_scale * z_norm
-    for copy in ys:
-        copy.wait_recv()
-    before = jnp.zeros((share, dv), F32)
-    for j in range(ny):
-        before = y_scales[j][0] * before + y_scales[j][1] * y_in[j].astype(F32)
-    for j in range(nz):
-        e_buf[j] = (e_scales[j][0] * before + e_scales[j][1] * p_buf[j]).astype(BF16)
-    es = []
-    for d in order:
-        peer = lax.rem(z + d, nz)
-        copy = remote(e_buf.at[peer], e_in.at[z], e_ss.at[d], e_rs.at[d], {"z": peer})
-        copy.start()
-        es.append(copy)
-    e_in[z] = e_buf[z]
-    sends += es
 
     e_scale, l_scale, both_max = merge(chip_max, a_top, a_decay)
     both_norm = e_scale * enter_norm + l_scale * a_norm
     my_max, my_norm = jnp.where(first, chip_max, both_max), jnp.where(first, enter_norm, both_norm)
     write_info(finfo_out, jnp.where(first, both_norm, enter_norm), jnp.where(first, both_max, chip_max), a_decay, gate)
-    finish = [remote(finfo_out, finfo_in, f_ss.at[0], f_rs.at[0], partner), remote(f_out, f_in, f_ss.at[1], f_rs.at[1], partner)]
-    finish[0].start()
-    for copy in es:
-        copy.wait_recv()
-    for j in range(nz):
-        rows = pl.ds(j * share, share)
-        entering = e_in[j].astype(F32)
-        a_rows = jnp.where(first, own1[rows, :], pair_in[rows, :].astype(F32))
-        both = e_scale * entering + l_scale * a_rows
-        f_out[rows, :] = jnp.where(first, both, entering).astype(BF16)
-        mine[rows, :] = jnp.where(first, entering, both).astype(BF16)
-    finish[1].start()
-    sends += finish
-
-    def readout(s, carry, norm, top):
+    ahead = remote(finfo_out, finfo_in, fi_ss.at[0], fi_rs.at[0], partner)
+    ahead.start()
+    sends.append(ahead)
+
+    es = []
+    for h in range(chunks):
+        for copy in ys[h]:
+            copy.wait_recv()
+        before = jnp.zeros((share, wide), F32)
+        for j in range(ny):
+            before = y_scales[j][0] * before + y_scales[j][1] * y_in[h, j].astype(F32)
+        for j in range(nz):
+            e_buf[h, j] = (e_scales[j][0] * before + e_scales[j][1] * p_buf[h, j]).astype(BF16)
+        es.append([])
+        for d in order:
+            peer = lax.rem(z + d, nz)
+            copy = remote(e_buf.at[h, peer], e_in.at[h, z], e_ss.at[h, d], e_rs.at[h, d], {"z": peer})
+            copy.start()
+            es[h].append(copy)
+        e_in[h, z] = e_buf[h, z]
+        sends += es[h]
+
+    def factors(s, norm, top):
         for r in range(2):
             rows = pl.ds(r * half, half)
-            q = q_buf[s, rows, :]
-            carried = dot(q, carry[...])
-            carried_den = jnp.sum(q.astype(F32) * norm, axis=1, keepdims=True)
+            carried_den = jnp.sum(q_buf[s, rows, :].astype(F32) * norm, axis=1, keepdims=True)
             b_top = bmax_buf[s, rows, :]
             stabilizer = jnp.maximum(b_top, top)
             a, k = jnp.exp(b_top - stabilizer), jnp.exp(top - stabilizer)
             den = a * den_buf[s, rows, :] + k * carried_den
             inverse = 1.0 / jnp.maximum(jnp.abs(den), 1.0)
-            hid[rows, s * dv : (s + 1) * dv] = ((a * inverse) * num_buf[s, rows, :] + (k * inverse) * carried).astype(BF16)
-
-    readout(1, mine, my_norm, my_max)
-    finish[0].wait_recv()
+            bmax_buf[s, rows, :] = a * inverse
+            den_buf[s, rows, :] = k * inverse
+
+    factors(1, my_norm, my_max)
+    ahead.wait_recv()
     other_norm, other_max, unused_decay, other_gate = read_info(finfo_in, 0)
     scale = 1.0 / (tokens * ny * nz * 2)
-    kept, got = (gate * scale)[0, 0], (other_gate * scale)[0, 0]
-    gate_ref[0] = jnp.where(first, kept, got)
-    gate_ref[1] = jnp.where(first, got, kept)
-    finish[1].wait_recv()
-    readout(0, f_in, other_norm, other_max)
-
-    step = 256
-    quarter = tokens // 4
-
-    def project(i, part, store):
-        def body(n, carry):
-            at = pl.ds(pl.multiple_of(n * step, step), step)
-            out = dot(hid[part * half : (part + 1) * half, :], w_buf[i, :, at])
-            store(part, at, out)
-            return carry
-
-        lax.fori_loop(0, cols // step, body, 0)
-
-    def to(buf):
-        def store(part, at, out):
-            for r in range(2):
-                buf[2 * part + r, :, at] = out[r * quarter : (r + 1) * quarter].astype(buf.dtype)
-
-        return store
+    lane = lax.broadcasted_iota(jnp.int32, (1, 2), 1)
+    gate_ref[...] = jnp.where(lane == c, gate, other_gate) * scale
+    factors(0, other_norm, other_max)
+
+    def readout(s, h, carry):
+        for r in range(2):
+            rows = pl.ds(r * half, half)
+            carried = dot(q_buf[s, rows, :], carry)
+            own = num_buf[s, rows, h * wide : (h + 1) * wide]
+            at = s * dv + h * wide
+            hid[rows, at : at + wide] = (bmax_buf[s, rows, :] * own + den_buf[s, rows, :] * carried).astype(BF16)
+
+    finish = []
+    for h in range(chunks):
+        for copy in es[h]:
+            copy.wait_recv()
+        for j in range(nz):
+            rows = pl.ds(j * share, share)
+            entering = e_in[h, j].astype(F32)
+            a_rows = jnp.where(first, own1[rows, h * wide : (h + 1) * wide], pair_in[rows, h * wide : (h + 1) * wide].astype(F32))
+            both = e_scale * entering + l_scale * a_rows
+            f_out[h, rows, :] = jnp.where(first, both, entering).astype(BF16)
+            mine[h, rows, :] = jnp.where(first, entering, both).astype(BF16)
+        copy = remote(f_out.at[h], f_in.at[h], f_ss.at[h], f_rs.at[h], partner)
+        copy.start()
+        finish.append(copy)
+        readout(1, h, mine[h])
+    sends += finish
+    for h in range(chunks):
+        finish[h].wait_recv()
+        readout(0, h, f_in[h])
+
+    def piece(i, part, n):
+        return dot(hid[part * half : (part + 1) * half, :], w_buf[i, :, n * step : (n + 1) * step])
 
     def ship(src, dst, ss, rs, r, peer):
         copy = remote(src.at[r], dst.at[r], ss.at[r], rs.at[r], peer)
         copy.start()
         return copy
 
-    for i in range(2):
-        w_loads[i].wait()
-    stage1 = [None] * 4
-    for part in range(2):
-        project(0, part, to(s1_out))
-        for r in (2 * part, 2 * part + 1):
-            stage1[r] = ship(s1_out, s1_in, s1_ss, s1_rs, r, left if part == 0 else right)
-    direct = [None] * 4
-    for i, part, peer in ((1, 1, left), (2, 0, right)):
+    def loaded(i):
         w_loads[2 * i].wait()
         w_loads[2 * i + 1].wait()
-        project(i, part, to(dir_out))
-        for r in (2 * part, 2 * part + 1):
-            direct[r] = ship(dir_out, dir_in, dir_ss, dir_rs, r, peer)
-    project(1, 0, to(rel_p))
-    project(2, 1, to(rel_p))
-    relay = [None] * 4
-    for r in (0, 2, 1, 3):
-        if r == 1:
-            w_loads[6].wait()
-            w_loads[7].wait()
-            project(3, 0, to(own_p))
-            project(3, 1, to(own_p))
-        stage1[r].wait_recv()
-        rel_out[r] = (rel_p[r] + s1_in[r].astype(F32)).astype(BF16)
-        relay[r] = ship(rel_out, rel_in, rel_ss, rel_rs, r, left if r < 2 else right)
+
+    parts = cols // step
+    towards = (left, right)
+    stage1, direct, relay = [], [], []
+    loaded(0)
+    for n in range(parts):
+        for part in range(2):
+            r = 2 * n + part
+            s1_out[r] = piece(0, part, n).astype(BF16)
+            stage1.append(ship(s1_out, s1_in, s1_ss, s1_rs, r, towards[part]))
+    loaded(1)
+    loaded(2)
+    for n in range(parts):
+        for part in range(2):
+            r = 2 * n + part
+            dir_out[r] = piece(2 - part, part, n).astype(BF16)
+            direct.append(ship(dir_out, dir_in, dir_ss, dir_rs, r, towards[1 - part]))
+    for n in range(parts):
+        for part in range(2):
+            r = 2 * n + part
+            partial = piece(1 + part, part, n)
+            stage1[r].wait_recv()
+            rel_out[r] = (partial + s1_in[r].astype(F32)).astype(BF16)
+            relay.append(ship(rel_out, rel_in, rel_ss, rel_rs, r, towards[part]))
+    loaded(3)
+    for n in range(parts):
+        for part in range(2):
+            own_p[2 * n + part] = piece(3, part, n)
     sends += stage1 + direct + relay
-    outs = []
-    for r in (0, 2, 1, 3):
-        direct[r].wait_recv()
-        relay[r].wait_recv()
-        out_buf[r] = (own_p[r] + dir_in[r].astype(F32) + rel_in[r].astype(F32)).astype(BF16)
-        copy = pltpu.make_async_copy(out_buf.at[r], mixed_hbm.at[pl.ds(r * quarter, quarter), :], out_sem.at[r])
-        copy.start()
-        outs.append(copy)
+    for n in range(parts):
+        for part in range(2):
+            r = 2 * n + part
+            direct[r].wait_recv()
+            partial = own_p[r] + dir_in[r].astype(F32)
+            relay[r].wait_recv()
+            mixed_ref[part * half : (part + 1) * half, n * step : (n + 1) * step] = (partial + rel_in[r].astype(F32)).astype(BF16)
     for copy in sends:
         copy.wait_send()
-    for copy in outs:
-        copy.wait()
 
 
 def shards(queries, keys, values, forget_gate, input_gate, out_weight):
@@ -401,16 +413,17 @@
     ny, nz, nx = (lax.axis_size(a) for a in ("y", "z", "x"))
     cols = width // nx
     share = dk // nz
-    quarter = tokens // 4
-    any_space = pl.BlockSpec(memory_space=pl.ANY)
+    chunks, step = 4, 256
+    wide, count = dv // chunks, 2 * cols // step
+    any_space = pl.BlockSpec(memory_space=pltpu.HBM)
     dma = pltpu.SemaphoreType.DMA
     info = lambda n: pltpu.VMEM((n, 1, INFO), F32)
-    quad = lambda kind: pltpu.VMEM((4, quarter, cols), kind)
+    pieces = lambda kind: pltpu.VMEM((count, tokens // 2, step), kind)
     mixed, gate_mean = pl.pallas_call(
         functools.partial(kernel, (ny, nz, nx)),
-        out_shape=(jax.ShapeDtypeStruct((tokens, cols), BF16), jax.ShapeDtypeStruct((heads,), F32)),
+        out_shape=(pltpu.VMEM((tokens, cols), BF16), pltpu.VMEM((1, heads), F32)),
         in_specs=[any_space] * 6,
-        out_specs=(any_space, pl.BlockSpec(memory_space=pltpu.SMEM)),
+        out_specs=(pl.BlockSpec(memory_space=pltpu.VMEM), pl.BlockSpec(memory_space=pltpu.VMEM)),
         scratch_shapes=[
             pltpu.VMEM((2, tokens, dk), BF16),
             pltpu.VMEM((2, tokens, dk), BF16),
@@ -424,42 +437,41 @@
             pltpu.VMEM((dk, dv), BF16),
             info(1),
             info(1),
-            pltpu.VMEM((nz, share, dv), BF16),
-            pltpu.VMEM((nz, share, dv), BF16),
+            pltpu.VMEM((chunks, nz, share, wide), BF16),
+            pltpu.VMEM((chunks, nz, share, wide), BF16),
             info(1),
             info(nz),
-            pltpu.VMEM((nz, share, dv), F32),
-            pltpu.VMEM((share, dv), BF16),
-            pltpu.VMEM((ny, share, dv), BF16),
+            pltpu.VMEM((chunks, nz, share, wide), F32),
+            pltpu.VMEM((chunks, share, wide), BF16),
+            pltpu.VMEM((chunks, ny, share, wide), BF16),
             info(1),
             info(ny),
-            pltpu.VMEM((nz, share, dv), BF16),
-            pltpu.VMEM((nz, share, dv), BF16),
-            pltpu.VMEM((dk, dv), BF16),
-            pltpu.VMEM((dk, dv), BF16),
-            info(1),
-            info(1),
-            pltpu.VMEM((dk, dv), BF16),
+            pltpu.VMEM((chunks, nz, share, wide), BF16),
+            pltpu.VMEM((chunks, nz, share, wide), BF16),
+            pltpu.VMEM((chunks, dk, wide), BF16),
+            pltpu.VMEM((chunks, dk, wide), BF16),
+            info(1),
+            info(1),
+            pltpu.VMEM((chunks, dk, wide), BF16),
             pltpu.VMEM((2, tokens, dv), F32),
             pltpu.VMEM((2, tokens, 1), F32),
             pltpu.VMEM((2, tokens, 1), F32),
             pltpu.VMEM((tokens, heads * dv), BF16),
-            quad(BF16), quad(BF16), quad(BF16), quad(BF16), quad(BF16), quad(BF16),
-            quad(F32), quad(F32), quad(BF16),
-            dma((8,)), dma((8,)), dma((4,)),
+            pieces(BF16), pieces(BF16), pieces(BF16), pieces(BF16), pieces(BF16), pieces(BF16), pieces(F32),
+            dma((8,)), dma((8,)),
             dma((2,)), dma((2,)),
-            dma((nz,)), dma((nz,)), dma((nz,)), dma((nz,)),
-            dma((ny,)), dma((ny,)), dma((ny,)), dma((ny,)),
-            dma((nz,)), dma((nz,)),
-            dma((2,)), dma((2,)),
-            dma((4,)), dma((4,)), dma((4,)), dma((4,)), dma((4,)), dma((4,)),
+            dma((chunks, nz)), dma((chunks, nz)), dma((nz,)), dma((nz,)),
+            dma((chunks, ny)), dma((chunks, ny)), dma((ny,)), dma((ny,)),
+            dma((chunks, nz)), dma((chunks, nz)),
+            dma((chunks,)), dma((chunks,)), dma((1,)), dma((1,)),
+            dma((count,)), dma((count,)), dma((count,)), dma((count,)), dma((count,)), dma((count,)),
         ],
         compiler_params=pltpu.CompilerParams(
-            collective_id=0, has_side_effects=True, vmem_limit_bytes=60 * 1024 * 1024
+            collective_id=0, has_side_effects=True, vmem_limit_bytes=65000000
         ),
         name="mlstm_layer",
     )(queries, keys, values, forget_gate.T, input_gate.T, out_weight)
-    return mixed, gate_mean
+    return mixed, gate_mean.reshape(heads)
 
 
 def solution(mesh):

time: 79.3 us -> 72.1 us (0.909)
  Pallas kernels: 75.1 us -> 69.9 us
  local copies, waits for them, and re-layouts: 3.38 us -> 1.48 us
    pallas_call x1, Pallas kernels: 75.1 us -> 69.9 us  [shards(): pl.pallas_call(functools.partial(kernel, (ny, nz, nx)), out_shape=(pltpu....]
    unnamed x2, local copies, waits for them, and re-layouts: 3.38 us -> 1.48 us
where the time goes in v2:
time: 72.1 us; the launch traced here: 72 us
  Pallas kernels  69.9 us (97%)
  local copies, waits for them, and re-layouts  1.48 us (2%)
    pallas_call x1, Pallas kernels, shards(): pl.pallas_call(functools.partial(kernel, (ny, nz, nx)), out_shape=(pltpu....  69.9 us
    unnamed x2, local copies, waits for them, and re-layouts  1.48 us

profile of v2, /device:TPU:1, one launch (start us, length us, event | category | flops | bytes accessed | tf_op | source)
XLA Modules:
  0.0 72.0 jit_solution(2310270514380668349)
XLA Ops:
  0.6 69.9 %mlstm_layer.1 = (bf16[512,1024]{1,0:T(8,128)(2,1)S(1)}, f32[1,2]{1,0:T(1,128)S(1)}) custom-call(bf16[512,512]{1,0:T(8,128)(2,1)} %q_hbm.1, bf16[512,512]{1,0:T(8,128)(2,1)} %k_hbm.1, bf16[512,1024]{1,0:T(8,128)(2,1)} %v_hbm.1, f32[2,512]{1,0:T(2,128)} %bitcast.4, f32[2,512]{1,0:T(2,128)} %bitcast.5, bf16[1024,4096]{1,0:T(8,128)(2,1)} %w_hbm.1), custom_call_target="tpu_custom_call" | custom-call | tf_op jit(solution)/shard_map/mlstm_layer/pallas_call | solution.py:422
  70.5 1.0 %copy.10 = bf16[512,1024]{1,0:T(8,128)(2,1)} copy(bf16[512,1024]{1,0:T(8,128)(2,1)S(1)} %get-tuple-element.6) | data formatting | bytes 2097152
  71.5 0.5 copy.11

commit v3 on v2

--- a/solution.py
+++ b/solution.py
@@ -54,10 +54,10 @@
     p_buf, y_out, y_in, yinfo_out, yinfo,
     e_buf, e_in, f_out, f_in, finfo_out, finfo_in, mine,
     num_buf, bmax_buf, den_buf, hid,
-    s1_out, s1_in, dir_out, dir_in, rel_out, rel_in, own_p,
+    ag_in, acc,
     load_sem, w_sem,
     pair_ss, pair_rs, z_ss, z_rs, zi_ss, zi_rs, y_ss, y_rs, yi_ss, yi_rs, e_ss, e_rs, f_ss, f_rs, fi_ss, fi_rs,
-    s1_ss, s1_rs, dir_ss, dir_rs, rel_ss, rel_rs,
+    wx_ss, wx_rs, wy_ss, wy_rs, wf_ss, wf_rs, wp_ss, wp_rs, ag_ss, ag_rs, af_ss, af_rs,
 ):
     ny, nz, nx = sizes
     y, z, c, x = (lax.axis_index(a) for a in ("y", "z", "c", "x"))
@@ -65,8 +65,9 @@
     dk, dv = q_buf.shape[2], v_buf.shape[2]
     half = tokens // 2
     cols = w_buf.shape[2]
+    slab = w_buf.shape[1] // (2 * ny)
     share = dk // nz
-    chunks, wide, step = t_buf.shape[0], t_buf.shape[3], own_p.shape[2]
+    chunks, wide, step = t_buf.shape[0], t_buf.shape[3], acc.shape[2]
     first = c == 0
     heads = (1 - c, c)
 
@@ -90,21 +91,10 @@
     peers += [{"z": lax.rem(z + d, nz)} for d in range(1, nz)]
     peers += [{"y": lax.rem(y + d, ny)} for d in range(1, ny)]
     left, right = {"x": lax.rem(x + nx - 1, nx)}, {"x": lax.rem(x + 1, nx)}
-    peers += [left, right]
+    far = {"x": lax.rem(x + 2, nx)}
+    peers += [left, right, far]
     for peer in peers:
         pl.semaphore_signal(barrier, inc=1, device_id=peer, device_id_type=MESH)
-
-    targets = (lax.rem(x + 2, nx), lax.rem(x + nx - 1, nx), lax.rem(x + 1, nx), x)
-    w_loads = []
-    for i in range(4):
-        for s in range(2):
-            copy = pltpu.make_async_copy(
-                w_hbm.at[pl.ds(pl.multiple_of(heads[s] * dv, 128), dv), pl.ds(pl.multiple_of(targets[i] * cols, 128), cols)],
-                w_buf.at[i, pl.ds(s * dv, dv), :],
-                w_sem.at[2 * i + s],
-            )
-            copy.start()
-            w_loads.append(copy)
 
     loads[0].wait()
     loads[1].wait()
@@ -164,6 +154,20 @@
         copy.start()
     sends += pair
 
+    def slab_of(y_index, c_index):
+        return pl.multiple_of((y_index * 2 + c_index) * slab, slab)
+
+    mine_rows = pl.ds(slab_of(y, c), slab)
+    wx = []
+    for i, peer in ((0, right), (1, left), (2, far)):
+        copy = remote(
+            w_hbm.at[mine_rows, pl.ds(pl.multiple_of(peer["x"] * cols, 128), cols)], w_buf.at[i, mine_rows, :], wx_ss.at[i], wx_rs.at[i], peer
+        )
+        copy.start()
+        wx.append(copy)
+    sends += wx
+    w_own = pltpu.make_async_copy(w_hbm.at[:, pl.ds(pl.multiple_of(x * cols, 128), cols)], w_buf.at[3], w_sem.at[0])
+
     loads[4].wait()
     loads[5].wait()
     matrix1, norm1 = own_state(1)
@@ -202,6 +206,8 @@
         t_in[h, z] = t_buf[h, z]
         sends += zs[h]
     sends += zi
+
+    w_own.start()
 
     loads[6].wait()
     loads[7].wait()
@@ -307,6 +313,36 @@
         e_in[h, z] = e_buf[h, z]
         sends += es[h]
 
+    upward, downward = {"y": lax.rem(y + 1, ny)}, {"y": lax.rem(y + ny - 1, ny)}
+    w_pair = []
+
+    def to_partner(i, rows, n):
+        place = w_buf.at[i, rows, :]
+        copy = remote(place, place, wp_ss.at[n, i], wp_rs.at[n, i], partner)
+        copy.start()
+        w_pair.append(copy)
+
+    wy = [[], []]
+    for i in range(3):
+        wx[i].wait_recv()
+        place = w_buf.at[i, mine_rows, :]
+        for way, peer in ((0, upward), (1, downward)):
+            copy = remote(place, place, wy_ss.at[way, i], wy_rs.at[way, i], peer)
+            copy.start()
+            wy[way].append(copy)
+        to_partner(i, mine_rows, 0)
+    wf = [[], []]
+
+    def pass_weights(i):
+        for way, peer, source in ((0, upward, y + ny - 1), (1, downward, y + 1)):
+            wy[way][i].wait_recv()
+            start = slab_of(lax.rem(source, ny), c)
+            place = w_buf.at[i, pl.ds(pl.multiple_of(start + way * (slab // 2), slab // 2), slab // 2), :]
+            copy = remote(place, place, wf_ss.at[way, i], wf_rs.at[way, i], peer)
+            copy.start()
+            wf[way].append(copy)
+            to_partner(i, pl.ds(start, slab), 1 + way)
+
     def factors(s, norm, top):
         for r in range(2):
             rows = pl.ds(r * half, half)
@@ -332,8 +368,18 @@
             rows = pl.ds(r * half, half)
             carried = dot(q_buf[s, rows, :], carry)
             own = num_buf[s, rows, h * wide : (h + 1) * wide]
-            at = s * dv + h * wide
-            hid[rows, at : at + wide] = (bmax_buf[s, rows, :] * own + den_buf[s, rows, :] * carried).astype(BF16)
+            hid[s * chunks + h, rows, :] = (bmax_buf[s, rows, :] * own + den_buf[s, rows, :] * carried).astype(BF16)
+
+    ag = [{}, {}]
+    sequence = []
+
+    def gather(s, h):
+        r = s * chunks + h
+        sequence.append(r)
+        for way, peer in ((0, right), (1, left)):
+            copy = remote(hid.at[r], ag_in.at[way, r], ag_ss.at[way, r], ag_rs.at[way, r], peer)
+            copy.start()
+            ag[way][r] = copy
 
     finish = []
     for h in range(chunks):
@@ -350,58 +396,72 @@
         copy.start()
         finish.append(copy)
         readout(1, h, mine[h])
+        gather(1, h)
+        if h > 0:
+            finish[h - 1].wait_recv()
+            readout(0, h - 1, f_in[h - 1])
+            gather(0, h - 1)
     sends += finish
-    for h in range(chunks):
-        finish[h].wait_recv()
-        readout(0, h, f_in[h])
-
-    def piece(i, part, n):
-        return dot(hid[part * half : (part + 1) * half, :], w_buf[i, :, n * step : (n + 1) * step])
-
-    def ship(src, dst, ss, rs, r, peer):
-        copy = remote(src.at[r], dst.at[r], ss.at[r], rs.at[r], peer)
-        copy.start()
-        return copy
-
-    def loaded(i):
-        w_loads[2 * i].wait()
-        w_loads[2 * i + 1].wait()
+    finish[chunks - 1].wait_recv()
+    readout(0, chunks - 1, f_in[chunks - 1])
+    gather(0, chunks - 1)
+
+    def product(source, i, s, n, low, high):
+        hidden = [source[s * chunks + h] for h in range(low, high)]
+        left_side = hidden[0] if len(hidden) == 1 else jnp.concatenate(hidden, axis=1)
+        rows = pl.ds(pl.multiple_of(heads[s] * dv + low * wide, wide), (high - low) * wide)
+        return dot(left_side, w_buf[i, rows, n * step : (n + 1) * step])
 
     parts = cols // step
-    towards = (left, right)
-    stage1, direct, relay = [], [], []
-    loaded(0)
+    w_own.wait()
     for n in range(parts):
-        for part in range(2):
-            r = 2 * n + part
-            s1_out[r] = piece(0, part, n).astype(BF16)
-            stage1.append(ship(s1_out, s1_in, s1_ss, s1_rs, r, towards[part]))
-    loaded(1)
-    loaded(2)
+        acc[n] = product(hid, 3, 1, n, 0, chunks) + product(hid, 3, 0, n, 0, chunks)
+
+    passed_on = [{}, {}]
+
+    def pass_hidden(r):
+        for way, peer in ((0, right), (1, left)):
+            ag[way][r].wait_recv()
+            rows = pl.ds(way * half, half)
+            copy = remote(ag_in.at[way, r, rows, :], ag_in.at[2, r, rows, :], af_ss.at[way, r], af_rs.at[way, r], peer)
+            copy.start()
+            passed_on[way][r] = copy
+
+    plan = iter(sequence)
+    for i, count in ((0, 1), (1, 2), (2, 2)):
+        for _ in range(count):
+            pass_hidden(next(plan))
+        pass_weights(i)
+    for r in plan:
+        pass_hidden(r)
+    far_rows = pl.ds(slab_of(lax.rem(y + 2, ny), c), slab)
+    for i in range(3):
+        wf[0][i].wait_recv()
+        wf[1][i].wait_recv()
+        to_partner(i, far_rows, 3)
+    for copy in w_pair:
+        copy.wait_recv()
     for n in range(parts):
-        for part in range(2):
-            r = 2 * n + part
-            dir_out[r] = piece(2 - part, part, n).astype(BF16)
-            direct.append(ship(dir_out, dir_in, dir_ss, dir_rs, r, towards[1 - part]))
+        acc[n] += (product(ag_in.at[0], 0, 1, n, 0, chunks) + product(ag_in.at[0], 0, 0, n, 0, chunks)) + (
+            product(ag_in.at[1], 1, 1, n, 0, chunks) + product(ag_in.at[1], 1, 0, n, 0, chunks)
+        )
+
+    def arrived(s, low, high):
+        for h in range(low, high):
+            for way in range(2):
+                passed_on[way][s * chunks + h].wait_recv()
+
+    arrived(1, 0, chunks)
+    arrived(0, 0, chunks - 1)
     for n in range(parts):
-        for part in range(2):
-            r = 2 * n + part
-            partial = piece(1 + part, part, n)
-            stage1[r].wait_recv()
-            rel_out[r] = (partial + s1_in[r].astype(F32)).astype(BF16)
-            relay.append(ship(rel_out, rel_in, rel_ss, rel_rs, r, towards[part]))
-    loaded(3)
+        acc[n] += product(ag_in.at[2], 2, 1, n, 0, chunks) + product(ag_in.at[2], 2, 0, n, 0, chunks - 1)
+    arrived(0, chunks - 1, chunks)
     for n in range(parts):
-        for part in range(2):
-            own_p[2 * n + part] = piece(3, part, n)
-    sends += stage1 + direct + relay
-    for n in range(parts):
-        for part in range(2):
-            r = 2 * n + part
-            direct[r].wait_recv()
-            partial = own_p[r] + dir_in[r].astype(F32)
-            relay[r].wait_recv()
-            mixed_ref[part * half : (part + 1) * half, n * step : (n + 1) * step] = (partial + rel_in[r].astype(F32)).astype(BF16)
+        mixed_ref[:, n * step : (n + 1) * step] = (acc[n] + product(ag_in.at[2], 2, 0, n, chunks - 1, chunks)).astype(BF16)
+    for group in wy + wf + [w_pair]:
+        sends += group
+    for group in ag + passed_on:
+        sends += list(group.values())
     for copy in sends:
         copy.wait_send()
 
@@ -414,11 +474,10 @@
     cols = width // nx
     share = dk // nz
     chunks, step = 4, 256
-    wide, count = dv // chunks, 2 * cols // step
+    wide = dv // chunks
     any_space = pl.BlockSpec(memory_space=pltpu.HBM)
     dma = pltpu.SemaphoreType.DMA
     info = lambda n: pltpu.VMEM((n, 1, INFO), F32)
-    pieces = lambda kind: pltpu.VMEM((count, tokens // 2, step), kind)
     mixed, gate_mean = pl.pallas_call(
         functools.partial(kernel, (ny, nz, nx)),
         out_shape=(pltpu.VMEM((tokens, cols), BF16), pltpu.VMEM((1, heads), F32)),
@@ -456,15 +515,17 @@
             pltpu.VMEM((2, tokens, dv), F32),
             pltpu.VMEM((2, tokens, 1), F32),
             pltpu.VMEM((2, tokens, 1), F32),
-            pltpu.VMEM((tokens, heads * dv), BF16),
-            pieces(BF16), pieces(BF16), pieces(BF16), pieces(BF16), pieces(BF16), pieces(BF16), pieces(F32),
-            dma((8,)), dma((8,)),
+            pltpu.VMEM((2 * chunks, tokens, wide), BF16),
+            pltpu.VMEM((3, 2 * chunks, tokens, wide), BF16),
+            pltpu.VMEM((cols // step, tokens, step), F32),
+            dma((8,)), dma((1,)),
             dma((2,)), dma((2,)),
             dma((chunks, nz)), dma((chunks, nz)), dma((nz,)), dma((nz,)),
             dma((chunks, ny)), dma((chunks, ny)), dma((ny,)), dma((ny,)),
             dma((chunks, nz)), dma((chunks, nz)),
             dma((chunks,)), dma((chunks,)), dma((1,)), dma((1,)),
-            dma((count,)), dma((count,)), dma((count,)), dma((count,)), dma((count,)), dma((count,)),
+            dma((3,)), dma((3,)), dma((2, 3)), dma((2, 3)), dma((2, 3)), dma((2, 3)), dma((4, 3)), dma((4, 3)),
+            dma((2, 2 * chunks)), dma((2, 2 * chunks)), dma((2, 2 * chunks)), dma((2, 2 * chunks)),
         ],
         compiler_params=pltpu.CompilerParams(
             collective_id=0, has_side_effects=True, vmem_limit_bytes=65000000

time: 72.1 us -> 65.6 us (0.910)
  the two profiles are of different devices: /device:TPU:1 before, /device:TPU:16 now
where the time goes in v3:
time: 65.6 us; the launch traced here: 65.5 us
  Pallas kernels  63.4 us (97%)
  local copies, waits for them, and re-layouts  1.48 us (2%)
    pallas_call x1, Pallas kernels, shards(): pl.pallas_call(functools.partial(kernel, (ny, nz, nx)), out_shape=(pltpu....  63.4 us
    unnamed x2, local copies, waits for them, and re-layouts  1.48 us

profile of v3, /device:TPU:16, one launch (start us, length us, event | category | flops | bytes accessed | tf_op | source)
XLA Modules:
  0.0 65.5 jit_solution(5300997656805656467)
XLA Ops:
  0.6 63.4 %mlstm_layer.1 = (bf16[512,1024]{1,0:T(8,128)(2,1)S(1)}, f32[1,2]{1,0:T(1,128)S(1)}) custom-call(bf16[512,512]{1,0:T(8,128)(2,1)} %q_hbm.1, bf16[512,512]{1,0:T(8,128)(2,1)} %k_hbm.1, bf16[512,1024]{1,0:T(8,128)(2,1)} %v_hbm.1, f32[2,512]{1,0:T(2,128)} %bitcast.4, f32[2,512]{1,0:T(2,128)} %bitcast.5, bf16[1024,4096]{1,0:T(8,128)(2,1)} %w_hbm.1), custom_call_target="tpu_custom_call" | custom-call | tf_op jit(solution)/shard_map/mlstm_layer/pallas_call | solution.py:481
  64.1 1.0 %copy.10 = bf16[512,1024]{1,0:T(8,128)(2,1)} copy(bf16[512,1024]{1,0:T(8,128)(2,1)S(1)} %get-tuple-element.6) | data formatting | bytes 2097152
  65.0 0.5 copy.11

commit v4 on v3

--- a/solution.py
+++ b/solution.py
@@ -13,7 +13,7 @@
 F32 = jnp.float32
 BF16 = jnp.bfloat16
 LOW = -1e30
-INFO = 640
+INFO = 384
 
 
 def dot(a, b):
@@ -34,21 +34,20 @@
 
 def read_info(ref, j):
     row = ref[j]
-    return row[:, :256], row[:, 256:257], row[:, 384:385], row[:, 512:513]
+    return row[:, :256], row[:, 256:257], row[:, 288:289], row[:, 320:321]
 
 
 def write_info(ref, norm, top, decay, gate):
+    lane = lax.broadcasted_iota(jnp.int32, (1, 128), 1)
     ref[0, :, 0:256] = norm
-    ref[0, :, 256:384] = jnp.broadcast_to(top, (1, 128))
-    ref[0, :, 384:512] = jnp.broadcast_to(decay, (1, 128))
-    ref[0, :, 512:640] = jnp.broadcast_to(gate, (1, 128))
+    ref[0, :, 256:384] = jnp.where(lane < 32, top, jnp.where(lane < 64, decay, gate))
 
 
 def kernel(
     sizes,
     q_hbm, k_hbm, v_hbm, fg_hbm, ig_hbm, w_hbm,
     mixed_ref, gate_ref,
-    q_buf, k_buf, v_buf, fg_buf, ig_buf, w_buf, kt_buf,
+    q_buf, k_buf, v_buf, fg_buf, ig_buf, w_buf, kt_buf, wkt_buf,
     own1, pair_out, pair_in, pinfo_out, pinfo_in,
     t_buf, t_in, tinfo_out, tinfo,
     p_buf, y_out, y_in, yinfo_out, yinfo,
@@ -56,7 +55,7 @@
     num_buf, bmax_buf, den_buf, hid,
     ag_in, acc,
     load_sem, w_sem,
-    pair_ss, pair_rs, z_ss, z_rs, zi_ss, zi_rs, y_ss, y_rs, yi_ss, yi_rs, e_ss, e_rs, f_ss, f_rs, fi_ss, fi_rs,
+    pair_ss, pair_rs, pi_ss, pi_rs, z_ss, z_rs, zi_ss, zi_rs, y_ss, y_rs, yi_ss, yi_rs, e_ss, e_rs, f_ss, f_rs, fi_ss, fi_rs,
     wx_ss, wx_rs, wy_ss, wy_rs, wf_ss, wf_rs, wp_ss, wp_rs, ag_ss, ag_rs, af_ss, af_rs,
 ):
     ny, nz, nx = sizes
@@ -74,9 +73,7 @@
     loads = []
 
     def load(src, dst):
-        copy = pltpu.make_async_copy(src, dst, load_sem.at[len(loads)])
-        copy.start()
-        loads.append(copy)
+        loads.append(pltpu.make_async_copy(src, dst, load_sem.at[len(loads)]))
 
     load(fg_hbm, fg_buf)
     load(ig_hbm, ig_buf)
@@ -85,6 +82,9 @@
         load(v_hbm.at[:, pl.ds(pl.multiple_of(heads[s] * dv, 128), dv)], v_buf.at[s])
     for s in range(2):
         load(q_hbm.at[:, pl.ds(pl.multiple_of(heads[s] * dk, 128), dk)], q_buf.at[s])
+
+    for copy in loads[:4]:
+        copy.start()
 
     barrier = pltpu.get_barrier_semaphore()
     peers = [{"c": 1 - c}]
@@ -96,8 +96,10 @@
     for peer in peers:
         pl.semaphore_signal(barrier, inc=1, device_id=peer, device_id_type=MESH)
 
-    loads[0].wait()
-    loads[1].wait()
+    for copy in loads[:3]:
+        copy.wait()
+    for copy in loads[4:6]:
+        copy.start()
     fg, ig = fg_buf[...], ig_buf[...]
     lf = jnp.minimum(fg, 0.0) - jnp.log1p(jnp.exp(-jnp.abs(fg)))
     lf_rows = (jnp.where(first, lf[1:2], lf[0:1]), jnp.where(first, lf[0:1], lf[1:2]))
@@ -124,13 +126,14 @@
         weights.append(jnp.exp(b - b_top) * (dk**-0.5))
     gates = [jnp.sum(ig_rows[s], axis=1, keepdims=True) for s in range(2)]
 
-    def own_state(s):
+    def own_keys(s):
         kt = k_buf[s].T
         kt_buf[s] = kt
-        wkt = (kt.astype(F32) * weights[s]).astype(BF16)
-        matrix = dot(wkt, v_buf[s])
-        norm = jnp.sum(dot(three_rows(jnp.broadcast_to(weights[s], (8, tokens)), sub), k_buf[s]), axis=0, keepdims=True)
-        return matrix, norm
+        wkt_buf[s] = (kt.astype(F32) * weights[s]).astype(BF16)
+        return jnp.sum(dot(three_rows(jnp.broadcast_to(weights[s], (8, tokens)), sub), k_buf[s]), axis=0, keepdims=True)
+
+    def own_state(s, h):
+        return dot(wkt_buf[s], v_buf[s, :, h * wide : (h + 1) * wide])
 
     def remote(src, dst, ss, rs, peer):
         return pltpu.make_async_remote_copy(
@@ -139,20 +142,28 @@
 
     sends = []
 
-    loads[2].wait()
+    norm0 = own_keys(0)
+    write_info(pinfo_out, norm0, tops[0], decays[0], gates[0])
     loads[3].wait()
-    matrix0, norm0 = own_state(0)
-    pair_out[...] = matrix0.astype(BF16)
-    write_info(pinfo_out, norm0, tops[0], decays[0], gates[0])
+    for copy in loads[6:]:
+        copy.start()
+    pair_out[0] = own_state(0, 0).astype(BF16)
     pl.semaphore_wait(barrier, len(peers))
     partner = {"c": 1 - c}
-    pair = [
-        remote(pinfo_out, pinfo_in, pair_ss.at[0], pair_rs.at[0], partner),
-        remote(pair_out, pair_in, pair_ss.at[1], pair_rs.at[1], partner),
-    ]
-    for copy in pair:
-        copy.start()
-    sends += pair
+    pair_info = remote(pinfo_out, pinfo_in, pi_ss.at[0], pi_rs.at[0], partner)
+    pair_info.start()
+    pair = []
+
+    def send_pair(h):
+        copy = remote(pair_out.at[h], pair_in.at[h], pair_ss.at[h], pair_rs.at[h], partner)
+        copy.start()
+        pair.append(copy)
+
+    send_pair(0)
+    for h in range(1, chunks):
+        pair_out[h] = own_state(0, h).astype(BF16)
+        send_pair(h)
+    sends += [pair_info] + pair
 
     def slab_of(y_index, c_index):
         return pl.multiple_of((y_index * 2 + c_index) * slab, slab)
@@ -169,11 +180,11 @@
     w_own = pltpu.make_async_copy(w_hbm.at[:, pl.ds(pl.multiple_of(x * cols, 128), cols)], w_buf.at[3], w_sem.at[0])
 
     loads[4].wait()
+    norm1 = own_keys(1)
     loads[5].wait()
-    matrix1, norm1 = own_state(1)
-    own1[...] = matrix1
-
-    pair[0].wait_recv()
+    own1[0] = own_state(1, 0)
+
+    pair_info.wait_recv()
     in_norm, in_top, in_decay, in_gate = read_info(pinfo_in, 0)
     a_top, a_norm = jnp.where(first, tops[1], in_top), jnp.where(first, norm1, in_norm)
     a_decay = jnp.where(first, decays[1], in_decay)
@@ -190,13 +201,14 @@
         zi.append(copy)
     tinfo[z] = tinfo_out[0]
     own_scale, in_scale = jnp.where(first, e_scale, l_scale), jnp.where(first, l_scale, e_scale)
-    pair[1].wait_recv()
     zs = []
     for h in range(chunks):
-        at = pl.ds(h * wide, wide)
+        if h > 0:
+            own1[h] = own_state(1, h)
+        pair[h].wait_recv()
         for j in range(nz):
             rows = pl.ds(j * share, share)
-            t_buf[h, j] = (own_scale * own1[rows, at] + in_scale * pair_in[rows, at].astype(F32)).astype(BF16)
+            t_buf[h, j] = (own_scale * own1[h, rows, :] + in_scale * pair_in[h, rows, :].astype(F32)).astype(BF16)
         zs.append([])
         for d in order:
             peer = lax.rem(z + d, nz)
@@ -388,7 +400,7 @@
         for j in range(nz):
             rows = pl.ds(j * share, share)
             entering = e_in[h, j].astype(F32)
-            a_rows = jnp.where(first, own1[rows, h * wide : (h + 1) * wide], pair_in[rows, h * wide : (h + 1) * wide].astype(F32))
+            a_rows = jnp.where(first, own1[h, rows, :], pair_in[h, rows, :].astype(F32))
             both = e_scale * entering + l_scale * a_rows
             f_out[h, rows, :] = jnp.where(first, both, entering).astype(BF16)
             mine[h, rows, :] = jnp.where(first, entering, both).astype(BF16)
@@ -464,6 +476,14 @@
         sends += list(group.values())
     for copy in sends:
         copy.wait_send()
+
+
+def put_out(mixed_ref, gate_ref, mixed_hbm, gate_hbm, sems):
+    copies = [pltpu.make_async_copy(mixed_ref, mixed_hbm, sems.at[0]), pltpu.make_async_copy(gate_ref, gate_hbm, sems.at[1])]
+    for copy in copies:
+        copy.start()
+    for copy in copies:
+        copy.wait()
 
 
 def shards(queries, keys, values, forget_gate, input_gate, out_weight):
@@ -491,9 +511,10 @@
             pltpu.VMEM((heads, tokens), F32),
             pltpu.VMEM((4, heads * dv, cols), BF16),
             pltpu.VMEM((2, dk, tokens), BF16),
-            pltpu.VMEM((dk, dv), F32),
-            pltpu.VMEM((dk, dv), BF16),
-            pltpu.VMEM((dk, dv), BF16),
+            pltpu.VMEM((2, dk, tokens), BF16),
+            pltpu.VMEM((chunks, dk, wide), F32),
+            pltpu.VMEM((chunks, dk, wide), BF16),
+            pltpu.VMEM((chunks, dk, wide), BF16),
             info(1),
             info(1),
             pltpu.VMEM((chunks, nz, share, wide), BF16),
@@ -519,7 +540,7 @@
             pltpu.VMEM((3, 2 * chunks, tokens, wide), BF16),
             pltpu.VMEM((cols // step, tokens, step), F32),
             dma((8,)), dma((1,)),
-            dma((2,)), dma((2,)),
+            dma((chunks,)), dma((chunks,)), dma((1,)), dma((1,)),
             dma((chunks, nz)), dma((chunks, nz)), dma((nz,)), dma((nz,)),
             dma((chunks, ny)), dma((chunks, ny)), dma((ny,)), dma((ny,)),
             dma((chunks, nz)), dma((chunks, nz)),
@@ -532,6 +553,16 @@
         ),
         name="mlstm_layer",
     )(queries, keys, values, forget_gate.T, input_gate.T, out_weight)
+    in_vmem = pl.BlockSpec(memory_space=pltpu.VMEM)
+    mixed, gate_mean = pl.pallas_call(
+        put_out,
+        out_shape=(jax.ShapeDtypeStruct((tokens, cols), BF16), jax.ShapeDtypeStruct((1, heads), F32)),
+        in_specs=[in_vmem, in_vmem],
+        out_specs=(any_space, any_space),
+        scratch_shapes=[dma((2,))],
+        compiler_params=pltpu.CompilerParams(vmem_limit_bytes=4 * 1024 * 1024),
+        name="put_out",
+    )(mixed, gate_mean)
     return mixed, gate_mean.reshape(heads)
 
 

time: 65.6 us -> 64.6 us (0.985)
  the two profiles are of different devices: /device:TPU:16 before, /device:TPU:1 now
where the time goes in v4:
time: 64.6 us; the launch traced here: 63.3 us
  Pallas kernels  62.7 us (97%)
    pallas_call x1, Pallas kernels, shards(): pl.pallas_call(functools.partial(kernel, (ny, nz, nx)), out_shape=(pltpu....  61.7 us

profile of v4, /device:TPU:1, one launch (start us, length us, event | category | flops | bytes accessed | tf_op | source)
XLA Modules:
  0.0 63.3 jit_solution(17593530838106931698)
XLA Ops:
  0.6 61.7 %mlstm_layer.1 = (bf16[512,1024]{1,0:T(8,128)(2,1)S(1)}, f32[1,2]{1,0:T(1,128)S(1)}) custom-call(bf16[512,512]{1,0:T(8,128)(2,1)} %q_hbm.1, bf16[512,512]{1,0:T(8,128)(2,1)} %k_hbm.1, bf16[512,1024]{1,0:T(8,128)(2,1)} %v_hbm.1, f32[2,512]{1,0:T(2,128)} %bitcast.3, f32[2,512]{1,0:T(2,128)} %bitcast.4, bf16[1024,4096]{1,0:T(8,128)(2,1)} %w_hbm.1), custom_call_target="tpu_custom_call" | custom-call | tf_op jit(solution)/shard_map/mlstm_layer/pallas_call | solution.py:501
  62.4 1.0 %put_out.1 = (bf16[512,1024]{1,0:T(8,128)(2,1)}, f32[1,2]{1,0:T(1,128)}) custom-call(bf16[512,1024]{1,0:T(8,128)(2,1)S(1)} %get-tuple-element.6.mixed_ref, f32[1,2]{1,0:T(1,128)S(1)} %get-tuple-element.7.gate_ref), custom_call_target="tpu_custom_call" | custom-call | tf_op jit(solution)/shard_map/put_out/pallas_call | solution.py:557

commit v5 on v4

--- a/solution.py
+++ b/solution.py
@@ -47,7 +47,7 @@
     sizes,
     q_hbm, k_hbm, v_hbm, fg_hbm, ig_hbm, w_hbm,
     mixed_ref, gate_ref,
-    q_buf, k_buf, v_buf, fg_buf, ig_buf, w_buf, kt_buf, wkt_buf,
+    q_buf, k_buf, v_buf, fg_buf, ig_buf, w_buf, kt_buf, wkt_buf, upper,
     own1, pair_out, pair_in, pinfo_out, pinfo_in,
     t_buf, t_in, tinfo_out, tinfo,
     p_buf, y_out, y_in, yinfo_out, yinfo,
@@ -55,8 +55,7 @@
     num_buf, bmax_buf, den_buf, hid,
     ag_in, acc,
     load_sem, w_sem,
-    pair_ss, pair_rs, pi_ss, pi_rs, z_ss, z_rs, zi_ss, zi_rs, y_ss, y_rs, yi_ss, yi_rs, e_ss, e_rs, f_ss, f_rs, fi_ss, fi_rs,
-    wx_ss, wx_rs, wy_ss, wy_rs, wf_ss, wf_rs, wp_ss, wp_rs, ag_ss, ag_rs, af_ss, af_rs,
+    one_ss, one_rs, group_ss, group_rs, pair_rs, z_rs, y_rs, e_rs, f_rs, wy_rs, ag_rs, af_rs,
 ):
     ny, nz, nx = sizes
     y, z, c, x = (lax.axis_index(a) for a in ("y", "z", "c", "x"))
@@ -68,6 +67,7 @@
     share = dk // nz
     chunks, wide, step = t_buf.shape[0], t_buf.shape[3], acc.shape[2]
     first = c == 0
+    partner = {"c": 1 - c}
     heads = (1 - c, c)
 
     loads = []
@@ -96,6 +96,11 @@
     for peer in peers:
         pl.semaphore_signal(barrier, inc=1, device_id=peer, device_id_type=MESH)
 
+    upper[...] = (
+        (lax.broadcasted_iota(jnp.int32, (tokens, tokens), 0) <= lax.broadcasted_iota(jnp.int32, (tokens, tokens), 1))
+        .astype(F32)
+        .astype(BF16)
+    )
     for copy in loads[:3]:
         copy.wait()
     for copy in loads[4:6]:
@@ -105,15 +110,12 @@
     lf_rows = (jnp.where(first, lf[1:2], lf[0:1]), jnp.where(first, lf[0:1], lf[1:2]))
     ig_rows = (jnp.where(first, ig[1:2], ig[0:1]), jnp.where(first, ig[0:1], ig[1:2]))
     sub = lax.broadcasted_iota(jnp.int32, (8, tokens), 0)
-    upper = (
-        lax.broadcasted_iota(jnp.int32, (tokens, tokens), 0) <= lax.broadcasted_iota(jnp.int32, (tokens, tokens), 1)
-    ).astype(F32).astype(BF16)
     stacked = jnp.where(
         sub < 4,
         three_rows(jnp.broadcast_to(lf_rows[0], (8, tokens)), sub).astype(F32),
         three_rows(jnp.broadcast_to(lf_rows[1], (8, tokens)), sub - 4).astype(F32),
     ).astype(BF16)
-    cums = dot(stacked, upper)
+    cums = dot(stacked, upper[...])
     b_rows, decays, tops, weights = [], [], [], []
     for s in range(2):
         cum = jnp.sum(cums[4 * s : 4 * s + 4], axis=0, keepdims=True)
@@ -140,7 +142,11 @@
             src_ref=src, dst_ref=dst, send_sem=ss, recv_sem=rs, device_id=peer, device_id_type=MESH
         )
 
-    sends = []
+    def landed(place, sem):
+        remote(place, place, sem, sem, partner).wait_recv()
+
+    def left_here(place, sem):
+        remote(place, place, sem, sem, partner).wait_send()
 
     norm0 = own_keys(0)
     write_info(pinfo_out, norm0, tops[0], decays[0], gates[0])
@@ -149,13 +155,12 @@
         copy.start()
     pair_out[0] = own_state(0, 0).astype(BF16)
     pl.semaphore_wait(barrier, len(peers))
-    partner = {"c": 1 - c}
-    pair_info = remote(pinfo_out, pinfo_in, pi_ss.at[0], pi_rs.at[0], partner)
+    pair_info = remote(pinfo_out, pinfo_in, one_ss.at[0], one_rs.at[0], partner)
     pair_info.start()
     pair = []
 
     def send_pair(h):
-        copy = remote(pair_out.at[h], pair_in.at[h], pair_ss.at[h], pair_rs.at[h], partner)
+        copy = remote(pair_out.at[h], pair_in.at[h], group_ss.at[0], pair_rs.at[h], partner)
         copy.start()
         pair.append(copy)
 
@@ -163,20 +168,16 @@
     for h in range(1, chunks):
         pair_out[h] = own_state(0, h).astype(BF16)
         send_pair(h)
-    sends += [pair_info] + pair
 
     def slab_of(y_index, c_index):
         return pl.multiple_of((y_index * 2 + c_index) * slab, slab)
 
     mine_rows = pl.ds(slab_of(y, c), slab)
-    wx = []
     for i, peer in ((0, right), (1, left), (2, far)):
         copy = remote(
-            w_hbm.at[mine_rows, pl.ds(pl.multiple_of(peer["x"] * cols, 128), cols)], w_buf.at[i, mine_rows, :], wx_ss.at[i], wx_rs.at[i], peer
+            w_hbm.at[mine_rows, pl.ds(pl.multiple_of(peer["x"] * cols, 128), cols)], w_buf.at[i, mine_rows, :], group_ss.at[1], group_rs.at[0], peer
         )
         copy.start()
-        wx.append(copy)
-    sends += wx
     w_own = pltpu.make_async_copy(w_hbm.at[:, pl.ds(pl.multiple_of(x * cols, 128), cols)], w_buf.at[3], w_sem.at[0])
 
     loads[4].wait()
@@ -193,34 +194,12 @@
     e_scale, l_scale, chip_top = merge(a_top, l_top, l_decay)
     chip_norm = e_scale * a_norm + l_scale * l_norm
     write_info(tinfo_out, chip_norm, chip_top, a_decay + l_decay, gates[1] + in_gate)
-    zi = []
     order = sorted(range(1, nz), key=lambda d: -min(d, nz - d))
     for d in order:
-        copy = remote(tinfo_out.at[0], tinfo.at[z], zi_ss.at[d], zi_rs.at[d], {"z": lax.rem(z + d, nz)})
-        copy.start()
-        zi.append(copy)
+        copy = remote(tinfo_out.at[0], tinfo.at[z], group_ss.at[2], group_rs.at[1], {"z": lax.rem(z + d, nz)})
+        copy.start()
     tinfo[z] = tinfo_out[0]
     own_scale, in_scale = jnp.where(first, e_scale, l_scale), jnp.where(first, l_scale, e_scale)
-    zs = []
-    for h in range(chunks):
-        if h > 0:
-            own1[h] = own_state(1, h)
-        pair[h].wait_recv()
-        for j in range(nz):
-            rows = pl.ds(j * share, share)
-            t_buf[h, j] = (own_scale * own1[h, rows, :] + in_scale * pair_in[h, rows, :].astype(F32)).astype(BF16)
-        zs.append([])
-        for d in order:
-            peer = lax.rem(z + d, nz)
-            copy = remote(t_buf.at[h, peer], t_in.at[h, z], z_ss.at[h, d], z_rs.at[h, d], {"z": peer})
-            copy.start()
-            zs[h].append(copy)
-        t_in[h, z] = t_buf[h, z]
-        sends += zs[h]
-    sends += zi
-
-    w_own.start()
-
     loads[6].wait()
     loads[7].wait()
 
@@ -238,11 +217,32 @@
             den_buf[s, rows, :] = jnp.sum(weighted, axis=1, keepdims=True)
             num_buf[s, rows, :] = dot(weighted.astype(BF16), v_buf[s, :span, :])
 
-    intra(1)
+    @pl.when(c == 0)
+    def _():
+        intra(1)
+
+    for h in range(chunks):
+        if h > 0:
+            own1[h] = own_state(1, h)
+        pair[h].wait_recv()
+        for j in range(nz):
+            rows = pl.ds(j * share, share)
+            t_buf[h, j] = (own_scale * own1[h, rows, :] + in_scale * pair_in[h, rows, :].astype(F32)).astype(BF16)
+        for d in order:
+            peer = lax.rem(z + d, nz)
+            copy = remote(t_buf.at[h, peer], t_in.at[h, z], group_ss.at[3], z_rs.at[h], {"z": peer})
+            copy.start()
+        t_in[h, z] = t_buf[h, z]
+
+    w_own.start()
+
+    @pl.when(c == 1)
+    def _():
+        intra(1)
+
     intra(0)
 
-    for copy in zi:
-        copy.wait_recv()
+    landed(tinfo.at[: nz - 1], group_rs.at[1])
     top, decay, norm, gate = jnp.full((1, 1), LOW, F32), jnp.zeros((1, 1), F32), jnp.zeros((1, dk), F32), jnp.zeros((1, 1), F32)
     z_norm, z_top, z_decay = norm, top, decay
     z_tops, z_decays, scales = [], [], []
@@ -258,33 +258,24 @@
         gate = gate + j_gate
         scales.append((e_scale, l_scale))
     write_info(yinfo_out, norm, top, decay, gate)
-    yi = []
     y_order = sorted(range(1, ny), key=lambda d: -min(d, ny - d))
     for d in y_order:
-        copy = remote(yinfo_out.at[0], yinfo.at[y], yi_ss.at[d], yi_rs.at[d], {"y": lax.rem(y + d, ny)})
-        copy.start()
-        yi.append(copy)
+        copy = remote(yinfo_out.at[0], yinfo.at[y], group_ss.at[4], group_rs.at[2], {"y": lax.rem(y + d, ny)})
+        copy.start()
     yinfo[y] = yinfo_out[0]
-    ys = []
     for h in range(chunks):
-        for copy in zs[h]:
-            copy.wait_recv()
+        landed(t_in.at[h, : nz - 1], z_rs.at[h])
         running = jnp.zeros((share, wide), F32)
         for j in range(nz):
             p_buf[h, j] = running
             running = scales[j][0] * running + scales[j][1] * t_in[h, j].astype(F32)
         y_out[h] = running.astype(BF16)
-        ys.append([])
         for d in y_order:
-            copy = remote(y_out.at[h], y_in.at[h, y], y_ss.at[h, d], y_rs.at[h, d], {"y": lax.rem(y + d, ny)})
-            copy.start()
-            ys[h].append(copy)
+            copy = remote(y_out.at[h], y_in.at[h, y], group_ss.at[5], y_rs.at[h], {"y": lax.rem(y + d, ny)})
+            copy.start()
         y_in[h, y] = y_out[h]
-        sends += ys[h]
-    sends += yi
-
-    for copy in yi:
-        copy.wait_recv()
+
+    landed(yinfo.at[: ny - 1], group_rs.at[2])
     top, decay, norm, gate = jnp.full((1, 1), LOW, F32), jnp.zeros((1, 1), F32), jnp.zeros((1, dk), F32), jnp.zeros((1, 1), F32)
     y_scales = []
     for j in range(ny):
@@ -303,57 +294,45 @@
     both_norm = e_scale * enter_norm + l_scale * a_norm
     my_max, my_norm = jnp.where(first, chip_max, both_max), jnp.where(first, enter_norm, both_norm)
     write_info(finfo_out, jnp.where(first, both_norm, enter_norm), jnp.where(first, both_max, chip_max), a_decay, gate)
-    ahead = remote(finfo_out, finfo_in, fi_ss.at[0], fi_rs.at[0], partner)
+    ahead = remote(finfo_out, finfo_in, one_ss.at[1], one_rs.at[1], partner)
     ahead.start()
-    sends.append(ahead)
-
-    es = []
+
     for h in range(chunks):
-        for copy in ys[h]:
-            copy.wait_recv()
+        landed(y_in.at[h, : ny - 1], y_rs.at[h])
         before = jnp.zeros((share, wide), F32)
         for j in range(ny):
             before = y_scales[j][0] * before + y_scales[j][1] * y_in[h, j].astype(F32)
         for j in range(nz):
             e_buf[h, j] = (e_scales[j][0] * before + e_scales[j][1] * p_buf[h, j]).astype(BF16)
-        es.append([])
         for d in order:
             peer = lax.rem(z + d, nz)
-            copy = remote(e_buf.at[h, peer], e_in.at[h, z], e_ss.at[h, d], e_rs.at[h, d], {"z": peer})
-            copy.start()
-            es[h].append(copy)
+            copy = remote(e_buf.at[h, peer], e_in.at[h, z], group_ss.at[6], e_rs.at[h], {"z": peer})
+            copy.start()
         e_in[h, z] = e_buf[h, z]
-        sends += es[h]
 
     upward, downward = {"y": lax.rem(y + 1, ny)}, {"y": lax.rem(y + ny - 1, ny)}
-    w_pair = []
-
-    def to_partner(i, rows, n):
+    def to_partner(i, rows):
         place = w_buf.at[i, rows, :]
-        copy = remote(place, place, wp_ss.at[n, i], wp_rs.at[n, i], partner)
-        copy.start()
-        w_pair.append(copy)
+        remote(place, place, group_ss.at[7], group_rs.at[3], partner).start()
 
     wy = [[], []]
+    landed(w_buf.at[:3, :slab, :], group_rs.at[0])
     for i in range(3):
-        wx[i].wait_recv()
         place = w_buf.at[i, mine_rows, :]
         for way, peer in ((0, upward), (1, downward)):
-            copy = remote(place, place, wy_ss.at[way, i], wy_rs.at[way, i], peer)
+            copy = remote(place, place, group_ss.at[8], wy_rs.at[way, i], peer)
             copy.start()
             wy[way].append(copy)
-        to_partner(i, mine_rows, 0)
-    wf = [[], []]
+        to_partner(i, mine_rows)
 
     def pass_weights(i):
         for way, peer, source in ((0, upward, y + ny - 1), (1, downward, y + 1)):
             wy[way][i].wait_recv()
             start = slab_of(lax.rem(source, ny), c)
             place = w_buf.at[i, pl.ds(pl.multiple_of(start + way * (slab // 2), slab // 2), slab // 2), :]
-            copy = remote(place, place, wf_ss.at[way, i], wf_rs.at[way, i], peer)
-            copy.start()
-            wf[way].append(copy)
-            to_partner(i, pl.ds(start, slab), 1 + way)
+            copy = remote(place, place, group_ss.at[9], group_rs.at[4], peer)
+            copy.start()
+            to_partner(i, pl.ds(start, slab))
 
     def factors(s, norm, top):
         for r in range(2):
@@ -389,14 +368,13 @@
         r = s * chunks + h
         sequence.append(r)
         for way, peer in ((0, right), (1, left)):
-            copy = remote(hid.at[r], ag_in.at[way, r], ag_ss.at[way, r], ag_rs.at[way, r], peer)
+            copy = remote(hid.at[r], ag_in.at[way, r], group_ss.at[10], ag_rs.at[way, r], peer)
             copy.start()
             ag[way][r] = copy
 
     finish = []
     for h in range(chunks):
-        for copy in es[h]:
-            copy.wait_recv()
+        landed(e_in.at[h, : nz - 1], e_rs.at[h])
         for j in range(nz):
             rows = pl.ds(j * share, share)
             entering = e_in[h, j].astype(F32)
@@ -404,7 +382,7 @@
             both = e_scale * entering + l_scale * a_rows
             f_out[h, rows, :] = jnp.where(first, both, entering).astype(BF16)
             mine[h, rows, :] = jnp.where(first, entering, both).astype(BF16)
-        copy = remote(f_out.at[h], f_in.at[h], f_ss.at[h], f_rs.at[h], partner)
+        copy = remote(f_out.at[h], f_in.at[h], group_ss.at[11], f_rs.at[h], partner)
         copy.start()
         finish.append(copy)
         readout(1, h, mine[h])
@@ -413,7 +391,6 @@
             finish[h - 1].wait_recv()
             readout(0, h - 1, f_in[h - 1])
             gather(0, h - 1)
-    sends += finish
     finish[chunks - 1].wait_recv()
     readout(0, chunks - 1, f_in[chunks - 1])
     gather(0, chunks - 1)
@@ -429,15 +406,15 @@
     for n in range(parts):
         acc[n] = product(hid, 3, 1, n, 0, chunks) + product(hid, 3, 0, n, 0, chunks)
 
-    passed_on = [{}, {}]
+    last = chunks - 1
 
     def pass_hidden(r):
+        group = 0 if r >= chunks else 2 if r == last else 1
         for way, peer in ((0, right), (1, left)):
             ag[way][r].wait_recv()
             rows = pl.ds(way * half, half)
-            copy = remote(ag_in.at[way, r, rows, :], ag_in.at[2, r, rows, :], af_ss.at[way, r], af_rs.at[way, r], peer)
-            copy.start()
-            passed_on[way][r] = copy
+            copy = remote(ag_in.at[way, r, rows, :], ag_in.at[2, r, rows, :], group_ss.at[12], af_rs.at[group], peer)
+            copy.start()
 
     plan = iter(sequence)
     for i, count in ((0, 1), (1, 2), (2, 2)):
@@ -447,35 +424,42 @@
     for r in plan:
         pass_hidden(r)
     far_rows = pl.ds(slab_of(lax.rem(y + 2, ny), c), slab)
+    landed(w_buf.at[:3, :slab, :], group_rs.at[4])
     for i in range(3):
-        wf[0][i].wait_recv()
-        wf[1][i].wait_recv()
-        to_partner(i, far_rows, 3)
-    for copy in w_pair:
-        copy.wait_recv()
+        to_partner(i, far_rows)
+    landed(w_buf.at[:3, : ny * slab, :], group_rs.at[3])
     for n in range(parts):
         acc[n] += (product(ag_in.at[0], 0, 1, n, 0, chunks) + product(ag_in.at[0], 0, 0, n, 0, chunks)) + (
             product(ag_in.at[1], 1, 1, n, 0, chunks) + product(ag_in.at[1], 1, 0, n, 0, chunks)
         )
 
-    def arrived(s, low, high):
-        for h in range(low, high):
-            for way in range(2):
-                passed_on[way][s * chunks + h].wait_recv()
-
-    arrived(1, 0, chunks)
-    arrived(0, 0, chunks - 1)
+    landed(ag_in.at[2, :chunks], af_rs.at[0])
+    landed(ag_in.at[2, :last], af_rs.at[1])
     for n in range(parts):
         acc[n] += product(ag_in.at[2], 2, 1, n, 0, chunks) + product(ag_in.at[2], 2, 0, n, 0, chunks - 1)
-    arrived(0, chunks - 1, chunks)
+    landed(ag_in.at[2, 0], af_rs.at[2])
     for n in range(parts):
         mixed_ref[:, n * step : (n + 1) * step] = (acc[n] + product(ag_in.at[2], 2, 0, n, chunks - 1, chunks)).astype(BF16)
-    for group in wy + wf + [w_pair]:
-        sends += group
-    for group in ag + passed_on:
-        sends += list(group.values())
-    for copy in sends:
-        copy.wait_send()
+    pair_info.wait_send()
+    ahead.wait_send()
+    for n, place in enumerate(
+        (
+            pair_out,
+            w_buf.at[:3, :slab, :],
+            tinfo.at[: nz - 1],
+            t_buf.at[:, : nz - 1],
+            yinfo.at[: ny - 1],
+            y_in.at[:, : ny - 1],
+            e_buf.at[:, : nz - 1],
+            w_buf.at[:3, : ny * slab, :],
+            w_buf.at[:3, : 2 * slab, :],
+            w_buf.at[:3, :slab, :],
+            ag_in.at[:2],
+            f_out,
+            ag_in.at[2],
+        )
+    ):
+        left_here(place, group_ss.at[n])
 
 
 def put_out(mixed_ref, gate_ref, mixed_hbm, gate_hbm, sems):
@@ -512,6 +496,7 @@
             pltpu.VMEM((4, heads * dv, cols), BF16),
             pltpu.VMEM((2, dk, tokens), BF16),
             pltpu.VMEM((2, dk, tokens), BF16),
+            pltpu.VMEM((tokens, tokens), BF16),
             pltpu.VMEM((chunks, dk, wide), F32),
             pltpu.VMEM((chunks, dk, wide), BF16),
             pltpu.VMEM((chunks, dk, wide), BF16),
@@ -540,13 +525,9 @@
             pltpu.VMEM((3, 2 * chunks, tokens, wide), BF16),
             pltpu.VMEM((cols // step, tokens, step), F32),
             dma((8,)), dma((1,)),
-            dma((chunks,)), dma((chunks,)), dma((1,)), dma((1,)),
-            dma((chunks, nz)), dma((chunks, nz)), dma((nz,)), dma((nz,)),
-            dma((chunks, ny)), dma((chunks, ny)), dma((ny,)), dma((ny,)),
-            dma((chunks, nz)), dma((chunks, nz)),
-            dma((chunks,)), dma((chunks,)), dma((1,)), dma((1,)),
-            dma((3,)), dma((3,)), dma((2, 3)), dma((2, 3)), dma((2, 3)), dma((2, 3)), dma((4, 3)), dma((4, 3)),
-            dma((2, 2 * chunks)), dma((2, 2 * chunks)), dma((2, 2 * chunks)), dma((2, 2 * chunks)),
+            dma((2,)), dma((2,)), dma((13,)), dma((5,)),
+            dma((chunks,)), dma((chunks,)), dma((chunks,)), dma((chunks,)), dma((chunks,)),
+            dma((2, 3)), dma((2, 2 * chunks)), dma((3,)),
         ],
         compiler_params=pltpu.CompilerParams(
             collective_id=0, has_side_effects=True, vmem_limit_bytes=65000000

time: 64.6 us -> 62 us (0.960)
  Pallas kernels: 62.7 us -> 60.5 us
    pallas_call x1, Pallas kernels: 61.7 us -> 59.5 us  [shards(): pl.pallas_call(functools.partial(kernel, (ny, nz, nx)), out_shape=(pltpu....]
where the time goes in v5:
time: 62 us; the launch traced here: 61.2 us
  Pallas kernels  60.5 us (98%)
  between operations  0.64 us (1%)
    pallas_call x1, Pallas kernels, shards(): pl.pallas_call(functools.partial(kernel, (ny, nz, nx)), out_shape=(pltpu....  59.5 us

profile of v5, /device:TPU:1, one launch (start us, length us, event | category | flops | bytes accessed | tf_op | source)
XLA Modules:
  0.0 61.2 jit_solution(14148894545307832443)
XLA Ops:
  0.6 59.5 %mlstm_layer.1 = (bf16[512,1024]{1,0:T(8,128)(2,1)S(1)}, f32[1,2]{1,0:T(1,128)S(1)}) custom-call(bf16[512,512]{1,0:T(8,128)(2,1)} %q_hbm.1, bf16[512,512]{1,0:T(8,128)(2,1)} %k_hbm.1, bf16[512,1024]{1,0:T(8,128)(2,1)} %v_hbm.1, f32[2,512]{1,0:T(2,128)} %bitcast.3, f32[2,512]{1,0:T(2,128)} %bitcast.4, bf16[1024,4096]{1,0:T(8,128)(2,1)} %w_hbm.1), custom_call_target="tpu_custom_call" | custom-call | tf_op jit(solution)/shard_map/mlstm_layer/pallas_call | solution.py:485
  60.2 1.0 %put_out.1 = (bf16[512,1024]{1,0:T(8,128)(2,1)}, f32[1,2]{1,0:T(1,128)}) custom-call(bf16[512,1024]{1,0:T(8,128)(2,1)S(1)} %get-tuple-element.6.mixed_ref, f32[1,2]{1,0:T(1,128)S(1)} %get-tuple-element.7.gate_ref), custom_call_target="tpu_custom_call" | custom-call | tf_op jit(solution)/shard_map/put_out/pallas_call | solution.py:538

commit v6 on v5

--- a/solution.py
+++ b/solution.py
@@ -196,7 +196,7 @@
     write_info(tinfo_out, chip_norm, chip_top, a_decay + l_decay, gates[1] + in_gate)
     order = sorted(range(1, nz), key=lambda d: -min(d, nz - d))
     for d in order:
-        copy = remote(tinfo_out.at[0], tinfo.at[z], group_ss.at[2], group_rs.at[1], {"z": lax.rem(z + d, nz)})
+        copy = remote(tinfo_out.at[0], tinfo.at[z], group_ss.at[3], group_rs.at[1], {"z": lax.rem(z + d, nz)})
         copy.start()
     tinfo[z] = tinfo_out[0]
     own_scale, in_scale = jnp.where(first, e_scale, l_scale), jnp.where(first, l_scale, e_scale)
@@ -230,7 +230,7 @@
             t_buf[h, j] = (own_scale * own1[h, rows, :] + in_scale * pair_in[h, rows, :].astype(F32)).astype(BF16)
         for d in order:
             peer = lax.rem(z + d, nz)
-            copy = remote(t_buf.at[h, peer], t_in.at[h, z], group_ss.at[3], z_rs.at[h], {"z": peer})
+            copy = remote(t_buf.at[h, peer], t_in.at[h, z], group_ss.at[0], z_rs.at[h], {"z": peer})
             copy.start()
         t_in[h, z] = t_buf[h, z]
 
@@ -271,7 +271,7 @@
             running = scales[j][0] * running + scales[j][1] * t_in[h, j].astype(F32)
         y_out[h] = running.astype(BF16)
         for d in y_order:
-            copy = remote(y_out.at[h], y_in.at[h, y], group_ss.at[5], y_rs.at[h], {"y": lax.rem(y + d, ny)})
+            copy = remote(y_out.at[h], y_in.at[h, y], group_ss.at[0], y_rs.at[h], {"y": lax.rem(y + d, ny)})
             copy.start()
         y_in[h, y] = y_out[h]
 
@@ -297,43 +297,6 @@
     ahead = remote(finfo_out, finfo_in, one_ss.at[1], one_rs.at[1], partner)
     ahead.start()
 
-    for h in range(chunks):
-        landed(y_in.at[h, : ny - 1], y_rs.at[h])
-        before = jnp.zeros((share, wide), F32)
-        for j in range(ny):
-            before = y_scales[j][0] * before + y_scales[j][1] * y_in[h, j].astype(F32)
-        for j in range(nz):
-            e_buf[h, j] = (e_scales[j][0] * before + e_scales[j][1] * p_buf[h, j]).astype(BF16)
-        for d in order:
-            peer = lax.rem(z + d, nz)
-            copy = remote(e_buf.at[h, peer], e_in.at[h, z], group_ss.at[6], e_rs.at[h], {"z": peer})
-            copy.start()
-        e_in[h, z] = e_buf[h, z]
-
-    upward, downward = {"y": lax.rem(y + 1, ny)}, {"y": lax.rem(y + ny - 1, ny)}
-    def to_partner(i, rows):
-        place = w_buf.at[i, rows, :]
-        remote(place, place, group_ss.at[7], group_rs.at[3], partner).start()
-
-    wy = [[], []]
-    landed(w_buf.at[:3, :slab, :], group_rs.at[0])
-    for i in range(3):
-        place = w_buf.at[i, mine_rows, :]
-        for way, peer in ((0, upward), (1, downward)):
-            copy = remote(place, place, group_ss.at[8], wy_rs.at[way, i], peer)
-            copy.start()
-            wy[way].append(copy)
-        to_partner(i, mine_rows)
-
-    def pass_weights(i):
-        for way, peer, source in ((0, upward, y + ny - 1), (1, downward, y + 1)):
-            wy[way][i].wait_recv()
-            start = slab_of(lax.rem(source, ny), c)
-            place = w_buf.at[i, pl.ds(pl.multiple_of(start + way * (slab // 2), slab // 2), slab // 2), :]
-            copy = remote(place, place, group_ss.at[9], group_rs.at[4], peer)
-            copy.start()
-            to_partner(i, pl.ds(start, slab))
-
     def factors(s, norm, top):
         for r in range(2):
             rows = pl.ds(r * half, half)
@@ -346,13 +309,49 @@
             bmax_buf[s, rows, :] = a * inverse
             den_buf[s, rows, :] = k * inverse
 
-    factors(1, my_norm, my_max)
-    ahead.wait_recv()
-    other_norm, other_max, unused_decay, other_gate = read_info(finfo_in, 0)
-    scale = 1.0 / (tokens * ny * nz * 2)
+    for h in range(chunks):
+        landed(y_in.at[h, : ny - 1], y_rs.at[h])
+        before = jnp.zeros((share, wide), F32)
+        for j in range(ny):
+            before = y_scales[j][0] * before + y_scales[j][1] * y_in[h, j].astype(F32)
+        for j in range(nz):
+            e_buf[h, j] = (e_scales[j][0] * before + e_scales[j][1] * p_buf[h, j]).astype(BF16)
+        for d in order:
+            peer = lax.rem(z + d, nz)
+            copy = remote(e_buf.at[h, peer], e_in.at[h, z], group_ss.at[0], e_rs.at[h], {"z": peer})
+            copy.start()
+        e_in[h, z] = e_buf[h, z]
+        if h == 0:
+            factors(1, my_norm, my_max)
+        if h == chunks - 2:
+            ahead.wait_recv()
+            other_norm, other_max, unused_decay, other_gate = read_info(finfo_in, 0)
+            factors(0, other_norm, other_max)
+
+    upward, downward = {"y": lax.rem(y + 1, ny)}, {"y": lax.rem(y + ny - 1, ny)}
+    def to_partner(i, rows):
+        place = w_buf.at[i, rows, :]
+        remote(place, place, group_ss.at[1], group_rs.at[3], partner).start()
+
+    def start_weights():
+        landed(w_buf.at[:3, :slab, :], group_rs.at[0])
+        for i in range(3):
+            place = w_buf.at[i, mine_rows, :]
+            for peer in (upward, downward):
+                remote(place, place, group_ss.at[1], wy_rs.at[i], peer).start()
+            to_partner(i, mine_rows)
+
+    def pass_weights(i):
+        landed(w_buf.at[i, : 2 * slab, :], wy_rs.at[i])
+        for way, peer, source in ((0, upward, y + ny - 1), (1, downward, y + 1)):
+            start = slab_of(lax.rem(source, ny), c)
+            place = w_buf.at[i, pl.ds(pl.multiple_of(start + way * (slab // 2), slab // 2), slab // 2), :]
+            copy = remote(place, place, group_ss.at[1], group_rs.at[4], peer)
+            copy.start()
+            to_partner(i, pl.ds(start, slab))
+
     lane = lax.broadcasted_iota(jnp.int32, (1, 2), 1)
-    gate_ref[...] = jnp.where(lane == c, gate, other_gate) * scale
-    factors(0, other_norm, other_max)
+    gate_ref[...] = jnp.where(lane == c, gate, other_gate) * (1.0 / (tokens * ny * nz * 2))
 
     def readout(s, h, carry):
         for r in range(2):
@@ -361,16 +360,14 @@
             own = num_buf[s, rows, h * wide : (h + 1) * wide]
             hid[s * chunks + h, rows, :] = (bmax_buf[s, rows, :] * own + den_buf[s, rows, :] * carried).astype(BF16)
 
-    ag = [{}, {}]
     sequence = []
 
     def gather(s, h):
         r = s * chunks + h
         sequence.append(r)
         for way, peer in ((0, right), (1, left)):
-            copy = remote(hid.at[r], ag_in.at[way, r], group_ss.at[10], ag_rs.at[way, r], peer)
+            copy = remote(hid.at[r], ag_in.at[way, r], group_ss.at[2], ag_rs.at[r], peer)
             copy.start()
-            ag[way][r] = copy
 
     finish = []
     for h in range(chunks):
@@ -382,11 +379,13 @@
             both = e_scale * entering + l_scale * a_rows
             f_out[h, rows, :] = jnp.where(first, both, entering).astype(BF16)
             mine[h, rows, :] = jnp.where(first, entering, both).astype(BF16)
-        copy = remote(f_out.at[h], f_in.at[h], group_ss.at[11], f_rs.at[h], partner)
+        copy = remote(f_out.at[h], f_in.at[h], group_ss.at[0], f_rs.at[h], partner)
         copy.start()
         finish.append(copy)
         readout(1, h, mine[h])
         gather(1, h)
+        if h == 0:
+            start_weights()
         if h > 0:
             finish[h - 1].wait_recv()
             readout(0, h - 1, f_in[h - 1])
@@ -410,10 +409,10 @@
 
     def pass_hidden(r):
         group = 0 if r >= chunks else 2 if r == last else 1
+        landed(ag_in.at[:2, r], ag_rs.at[r])
         for way, peer in ((0, right), (1, left)):
-            ag[way][r].wait_recv()
             rows = pl.ds(way * half, half)
-            copy = remote(ag_in.at[way, r, rows, :], ag_in.at[2, r, rows, :], group_ss.at[12], af_rs.at[group], peer)
+            copy = remote(ag_in.at[way, r, rows, :], ag_in.at[2, r, rows, :], group_ss.at[2], af_rs.at[group], peer)
             copy.start()
 
     plan = iter(sequence)
@@ -442,23 +441,8 @@
         mixed_ref[:, n * step : (n + 1) * step] = (acc[n] + product(ag_in.at[2], 2, 0, n, chunks - 1, chunks)).astype(BF16)
     pair_info.wait_send()
     ahead.wait_send()
-    for n, place in enumerate(
-        (
-            pair_out,
-            w_buf.at[:3, :slab, :],
-            tinfo.at[: nz - 1],
-            t_buf.at[:, : nz - 1],
-            yinfo.at[: ny - 1],
-            y_in.at[:, : ny - 1],
-            e_buf.at[:, : nz - 1],
-            w_buf.at[:3, : ny * slab, :],
-            w_buf.at[:3, : 2 * slab, :],
-            w_buf.at[:3, :slab, :],
-            ag_in.at[:2],
-            f_out,
-            ag_in.at[2],
-        )
-    ):
+    state_rows = (2 * dk * dv + 2 * (nz - 1) * share * dv + (ny - 1) * share * dv) // cols
+    for n, place in enumerate((w_buf.at[0, :state_rows, :], w_buf.at[:3], ag_in, tinfo.at[: nz - 1], yinfo.at[: ny - 1])):
         left_here(place, group_ss.at[n])
 
 
@@ -525,9 +509,9 @@
             pltpu.VMEM((3, 2 * chunks, tokens, wide), BF16),
             pltpu.VMEM((cols // step, tokens, step), F32),
             dma((8,)), dma((1,)),
-            dma((2,)), dma((2,)), dma((13,)), dma((5,)),
+            dma((2,)), dma((2,)), dma((5,)), dma((5,)),
             dma((chunks,)), dma((chunks,)), dma((chunks,)), dma((chunks,)), dma((chunks,)),
-            dma((2, 3)), dma((2, 2 * chunks)), dma((3,)),
+            dma((3,)), dma((2 * chunks,)), dma((3,)),
         ],
         compiler_params=pltpu.CompilerParams(
             collective_id=0, has_side_effects=True, vmem_limit_bytes=65000000

time: 62 us -> 61.8 us (level)
  no operation moved by 1% of the time
where the time goes in v6:
time: 61.8 us; the launch traced here: 61 us
  Pallas kernels  60.3 us (98%)
  between operations  0.64 us (1%)
    pallas_call x1, Pallas kernels, shards(): pl.pallas_call(functools.partial(kernel, (ny, nz, nx)), out_shape=(pltpu....  59.3 us

profile of v6, /device:TPU:1, one launch (start us, length us, event | category | flops | bytes accessed | tf_op | source)
XLA Modules:
  0.0 61.0 jit_solution(14542826395875760724)
XLA Ops:
  0.6 59.3 %mlstm_layer.1 = (bf16[512,1024]{1,0:T(8,128)(2,1)S(1)}, f32[1,2]{1,0:T(1,128)S(1)}) custom-call(bf16[512,512]{1,0:T(8,128)(2,1)} %q_hbm.1, bf16[512,512]{1,0:T(8,128)(2,1)} %k_hbm.1, bf16[512,1024]{1,0:T(8,128)(2,1)} %v_hbm.1, f32[2,512]{1,0:T(2,128)} %bitcast.3, f32[2,512]{1,0:T(2,128)} %bitcast.4, bf16[1024,4096]{1,0:T(8,128)(2,1)} %w_hbm.1), custom_call_target="tpu_custom_call" | custom-call | tf_op jit(solution)/shard_map/mlstm_layer/pallas_call | solution.py:469
  60.0 1.0 %put_out.1 = (bf16[512,1024]{1,0:T(8,128)(2,1)}, f32[1,2]{1,0:T(1,128)}) custom-call(bf16[512,1024]{1,0:T(8,128)(2,1)S(1)} %get-tuple-element.6.mixed_ref, f32[1,2]{1,0:T(1,128)S(1)} %get-tuple-element.7.gate_ref), custom_call_target="tpu_custom_call" | custom-call | tf_op jit(solution)/shard_map/put_out/pallas_call | solution.py:522

commit v7 on v6

--- a/solution.py
+++ b/solution.py
@@ -194,7 +194,7 @@
     e_scale, l_scale, chip_top = merge(a_top, l_top, l_decay)
     chip_norm = e_scale * a_norm + l_scale * l_norm
     write_info(tinfo_out, chip_norm, chip_top, a_decay + l_decay, gates[1] + in_gate)
-    order = sorted(range(1, nz), key=lambda d: -min(d, nz - d))
+    order = sorted(range(1, nz), key=lambda d: (-min(d, nz - d), -d))
     for d in order:
         copy = remote(tinfo_out.at[0], tinfo.at[z], group_ss.at[3], group_rs.at[1], {"z": lax.rem(z + d, nz)})
         copy.start()
@@ -375,15 +375,16 @@
         for j in range(nz):
             rows = pl.ds(j * share, share)
             entering = e_in[h, j].astype(F32)
-            a_rows = jnp.where(first, own1[h, rows, :], pair_in[h, rows, :].astype(F32))
-            both = e_scale * entering + l_scale * a_rows
-            f_out[h, rows, :] = jnp.where(first, both, entering).astype(BF16)
-            mine[h, rows, :] = jnp.where(first, entering, both).astype(BF16)
-        copy = remote(f_out.at[h], f_in.at[h], group_ss.at[0], f_rs.at[h], partner)
-        copy.start()
-        finish.append(copy)
+            mine[h, rows, :] = jnp.where(first, entering, e_scale * entering + l_scale * pair_in[h, rows, :].astype(F32)).astype(BF16)
         readout(1, h, mine[h])
         gather(1, h)
+        for j in range(nz):
+            rows = pl.ds(j * share, share)
+            entering = e_in[h, j].astype(F32)
+            f_out[h, rows, :] = jnp.where(first, e_scale * entering + l_scale * own1[h, rows, :], entering).astype(BF16)
+        copy = remote(f_out.at[h], f_in.at[h], group_ss.at[0], f_rs.at[h], partner)
+        copy.start()
+        finish.append(copy)
         if h == 0:
             start_weights()
         if h > 0:

time: 61.8 us -> 61.8 us (level)
  no operation moved by 1% of the time
where the time goes in v7:
time: 61.8 us; the launch traced here: 61.2 us
  Pallas kernels  60.6 us (98%)
  between operations  0.64 us (1%)
    pallas_call x1, Pallas kernels, shards(): pl.pallas_call(functools.partial(kernel, (ny, nz, nx)), out_shape=(pltpu....  59.6 us

profile of v7, /device:TPU:1, one launch (start us, length us, event | category | flops | bytes accessed | tf_op | source)
XLA Modules:
  0.0 61.2 jit_solution(9239445615774432795)
XLA Ops:
  0.6 59.6 %mlstm_layer.1 = (bf16[512,1024]{1,0:T(8,128)(2,1)S(1)}, f32[1,2]{1,0:T(1,128)S(1)}) custom-call(bf16[512,512]{1,0:T(8,128)(2,1)} %q_hbm.1, bf16[512,512]{1,0:T(8,128)(2,1)} %k_hbm.1, bf16[512,1024]{1,0:T(8,128)(2,1)} %v_hbm.1, f32[2,512]{1,0:T(2,128)} %bitcast.3, f32[2,512]{1,0:T(2,128)} %bitcast.4, bf16[1024,4096]{1,0:T(8,128)(2,1)} %w_hbm.1), custom_call_target="tpu_custom_call" | custom-call | tf_op jit(solution)/shard_map/mlstm_layer/pallas_call | solution.py:470
  60.2 1.0 %put_out.1 = (bf16[512,1024]{1,0:T(8,128)(2,1)}, f32[1,2]{1,0:T(1,128)}) custom-call(bf16[512,1024]{1,0:T(8,128)(2,1)S(1)} %get-tuple-element.6.mixed_ref, f32[1,2]{1,0:T(1,128)S(1)} %get-tuple-element.7.gate_ref), custom_call_target="tpu_custom_call" | custom-call | tf_op jit(solution)/shard_map/put_out/pallas_call | solution.py:523
